TPU v7x, 256 devices: a whole 4x4x8 slice. The times are simulated.
256 devices in a mesh: store: 16 (over x, y_hi, core), tp: 16 (over y_lo, z).
Axes of the slice: x: 4, y: 4 (y_hi: 2, y_lo: 2; y = y_hi * 2 + y_lo), z: 8, core: 2. Of those that a mesh axis runs over, the one named last changes fastest.
Arguments:
- hidden: bfloat16 [16, 576, 8192], P('store', None, 'tp'), may hold values from -300 to 300
- w_query: bfloat16 [8192, 4096], P(None, 'tp'), may hold values from -0.0625 to 0.0625
- w_keyvalue: bfloat16 [8192, 1024], P('tp'), may hold values from -0.1875 to 0.1875
- passage_cache: bfloat16 [64, 4, 384, 256], P('store'), may hold values from -400 to 400
- passage_ids: int32 [16, 8], replicated, may hold values from 0 to 63, as said below
- select_index: int32 [16, 576], P('store'), may hold values from 0 to 3071, as said below
- select_count: int32 [16], P('store'), may hold values from 288 to 576, as said below
Outputs:
- context: bfloat16 [16, 576, 4096], P('store', None, 'tp')
Inputs may be any that keep to these rules, and one draw needn't show every extreme that they name: `passage_ids`: the passages of one prompt lie in distinct shards of the pool, shard = id // 4. `select_index`: all entries of a row are distinct positions of the prompt; the first select_count[p] of row p are in increasing order, the others are ignored. `select_count`: some prompt of every draw has 576 selected tokens.
All inputs are finite; a program needn't handle non-finite values.
Results may differ from a plain program's by a relative error of at most 0.04.
Values may be sent and summed in bfloat16 or wider, within the bound.
A program may use at most 128 MiB of HBM per device.

v0:
```python
import jax
import jax.numpy as jnp
from jax import lax
from jax.sharding import Mesh
from jax.sharding import PartitionSpec as P

D = 8192
KV_HEADS = 4
HEAD_DIM = 128
PASSAGE = 384
PASSAGES = 8
SEQ = 3072
TP = ("tp_0", "tp_1")


ROPE_BASE = 1000000.0
EPSILON = 1e-06


def in_blocks(value, dim, length):
    shape = value.shape
    parts = value.reshape(*shape[:dim], length, shape[dim] // length, *shape[dim + 1 :])
    return jnp.moveaxis(parts, dim, 0)


def summed_on_arrival(value, axis, dim):
    parts = in_blocks(value, dim, lax.axis_size(axis))
    arrived = lax.all_to_all(parts, axis, split_axis=0, concat_axis=0, tiled=True)
    return arrived.astype(jnp.float32).sum(axis=0)


def from_partner(value, axis, bit):
    return lax.ppermute(value, axis, [(i, i ^ 1 << bit) for i in range(lax.axis_size(axis))])


def joined_along(parts, dim):
    shape = list(parts.shape[1:])
    shape[dim] *= parts.shape[0]
    return jnp.moveaxis(parts, 0, dim).reshape(shape)


def stacked_from(value, axes, sequence):
    parts = value[None]
    for k in sequence:
        parts = lax.all_gather(parts, axes[k], axis=0, tiled=True)
    held = [lax.axis_size(axes[k]) for k in reversed(sequence)]
    parts = parts.reshape(*held, *value.shape)
    turned = sorted(range(len(sequence)), key=lambda place: sequence[len(sequence) - 1 - place])
    return parts.transpose(*turned, *range(len(sequence), parts.ndim)).reshape(-1, *value.shape)


def gather_axes(value, axes, sequence, dim):
    return joined_along(stacked_from(value, axes, sequence), dim)


def rotate(vectors, positions):
    half_dim = vectors.shape[-1] // 2
    frequency = ROPE_BASE ** (-(jnp.arange(half_dim, dtype=jnp.float32) * 2.0) / vectors.shape[-1])
    angles = positions.astype(jnp.float32)[..., None] * frequency
    cosine = jnp.cos(angles)
    sine_part = jnp.sin(angles)
    front_half = vectors[..., :half_dim]
    back_half = vectors[..., half_dim:]
    return jnp.concatenate(
        [front_half * cosine - back_half * sine_part, back_half * cosine + front_half * sine_part],
        axis=-1,
    )


def local(hidden, w_query, w_keyvalue, passage_cache, passage_ids, select_index, select_count):
    tp_count = lax.axis_size(TP)
    group_width = tp_count // KV_HEADS
    tp_rank = lax.axis_index(TP)
    kv_head = tp_rank // group_width
    store_rank = lax.axis_index("store")
    local_heads = w_query.shape[1] // HEAD_DIM
    row_count = hidden.shape[1]
    pool_dev = passage_cache.shape[0]
    partial_kv = jnp.dot(hidden[0], w_keyvalue, preferred_element_type=jnp.float32)
    head_kv = summed_on_arrival(partial_kv.astype(jnp.bfloat16), TP, 1)
    levels = group_width.bit_length() - 1
    for level in range(levels):
        partner = from_partner(head_kv.astype(jnp.bfloat16), TP, level).astype(head_kv.dtype)
        upper = tp_rank // 2**level % 2 == 1
        head_kv = jnp.where(
            upper,
            jnp.concatenate([partner, head_kv], axis=1),
            jnp.concatenate([head_kv, partner], axis=1),
        )
    token_part = gather_axes(hidden, TP, (0, 1), 2)[0]
    widened = token_part.astype(jnp.float32)
    running = jnp.dot(token_part, w_query, preferred_element_type=jnp.float32)
    squares = jnp.sum(widened * widened, axis=-1)
    inverse_rms = lax.rsqrt(squares / D + EPSILON)
    positions = select_index[0]
    live_count = select_count[0]
    queries = rotate(
        (running * inverse_rms[:, None]).reshape(row_count, local_heads, HEAD_DIM),
        positions[:, None],
    )
    queries = (queries * HEAD_DIM ** (-0.5)).astype(jnp.bfloat16)
    key_value = head_kv * inverse_rms[:, None]
    new_keys = rotate(key_value[:, :HEAD_DIM], positions).astype(jnp.bfloat16)
    new_values = key_value[:, HEAD_DIM:].astype(jnp.bfloat16)
    head_cache = lax.dynamic_index_in_dim(passage_cache, kv_head, 1, keepdims=False)
    owners = passage_ids // pool_dev
    local_index = passage_ids % pool_dev
    matches = owners == store_rank
    local_slot = jnp.sum(jnp.where(matches, local_index, 0), axis=1)
    present = jnp.any(matches, axis=1)
    outgoing = jnp.take(head_cache, local_slot, axis=0) * present[:, None, None].astype(
        jnp.bfloat16
    )
    incoming = lax.all_to_all(outgoing, "store", split_axis=0, concat_axis=0, tiled=True)
    my_owners = lax.dynamic_index_in_dim(owners, store_rank, 0, keepdims=False)
    fetched = jnp.take(incoming, my_owners, axis=0)
    offsets = jnp.arange(PASSAGES) * PASSAGE
    old_keys = rotate(fetched[..., :HEAD_DIM].astype(jnp.float32), offsets[:, None]).astype(
        jnp.bfloat16
    )
    old_keys = old_keys.reshape(SEQ, HEAD_DIM)
    old_values = fetched[..., HEAD_DIM:].reshape(SEQ, HEAD_DIM)
    row_ids = jnp.arange(row_count, dtype=jnp.int32)
    target = jnp.where(row_ids < live_count, positions, SEQ)
    all_keys = old_keys.at[target].set(new_keys, mode="drop")
    all_values = old_values.at[target].set(new_values, mode="drop")
    allowed = jnp.arange(SEQ, dtype=jnp.int32)[None, :] <= positions[:, None]
    scores = jnp.einsum("rgd,sd->grs", queries, all_keys, preferred_element_type=jnp.float32)
    scores = jnp.where(allowed[None], scores, -jnp.inf)
    row_max = jnp.max(scores, axis=-1, keepdims=True)
    shifted = jnp.exp(scores - row_max)
    weight = (shifted / jnp.sum(shifted, axis=-1, keepdims=True)).astype(jnp.bfloat16)
    context = jnp.einsum("grs,sd->rgd", weight, all_values, preferred_element_type=jnp.float32)
    row_live = (row_ids < live_count)[:, None, None]
    context = jnp.where(row_live, context, 0.0)
    return context.reshape(1, row_count, local_heads * HEAD_DIM).astype(jnp.bfloat16)


def solution(mesh):
    split = Mesh(mesh.devices.reshape(mesh.shape["store"], 2, 8), ("store", "tp_0", "tp_1"))
    placed = (
        P("store", None, TP),
        P(None, TP),
        P(TP, None),
        P("store", None, None, None),
        P(),
        P("store", None),
        P("store"),
    )
    return jax.shard_map(
        local, mesh=split, in_specs=placed, out_specs=P("store", None, TP), check_vma=False
    )
```

profile of v0, /device:TPU:2, one launch (start us, length us, event | category | flops | bytes accessed | tf_op | source)
XLA Modules:
  0.0 258.2 jit_solution(8467378492987644100)
XLA Ops:
  7.3 32.6 %all-gather.5.cloned.1.call-done = bf16[2,576,512]{2,1,0:T(8,128)(2,1)} async-done(((bf16[1,576,512]{2,1,0:T(8,128)(2,1)}), bf16[2,576,512]{2,1,0:T(8,128)(2,1)}) %all-gather.5.cloned.1.call-update) | async-done | bytes 1179664 | tf_op jit(solution)/shard_map/all_gather | solution.py:45
  40.0 3.2 %convolution_convert_fusion = bf16[576,1024]{1,0:T(8,128)(2,1)} fusion(bf16[512,1024]{1,0:T(8,128)(2,1)} %param.9, bf16[1,576,512]{2,1,0:T(8,128)(2,1)} %param.7), kind=kOutput, calls=%fused_computation.19 | convolution fusion | flops 604569600 | bytes 2818048 | tf_op jit(solution)/shard_map/dot_general | solution.py:79
  43.2 2.4 copy.39
  45.6 7.2 %all-to-all-start.1 = ((bf16[16,576,64]{1,2,0:T(8,128)(2,1)}), bf16[16,576,64]{1,2,0:T(8,128)(2,1)}, u32[]{:S(2)}, u32[]{:S(2)}) async-start(bf16[16,576,64]{1,2,0:T(8,128)(2,1)} %bitcast.72), calls=%async_computation.1 | async-start | bytes 2621440 | tf_op jit(solution)/shard_map/all_to_all | solution.py:28
  52.9 0.9 dynamic-slice_bitcast_fusion
  53.8 2.0 gather_fusion
  55.8 2.0 select_multiply_fusion
  57.8 42.2 %all-to-all-done.1 = bf16[16,576,64]{1,2,0:T(8,128)(2,1)} async-done(((bf16[16,576,64]{1,2,0:T(8,128)(2,1)}), bf16[16,576,64]{1,2,0:T(8,128)(2,1)}, u32[]{:S(2)}, u32[]{:S(2)}) %all-to-all-start.1) | async-done | bytes 1179680 | tf_op jit(solution)/shard_map/all_to_all | solution.py:28
  100.1 7.3 %all-to-all-start = ((bf16[16,384,256]{2,1,0:T(8,128)(2,1)}), bf16[16,384,256]{2,1,0:T(8,128)(2,1)S(1)}, u32[]{:S(2)}, u32[]{:S(2)}) async-start(bf16[16,384,256]{2,1,0:T(8,128)(2,1)} %select_multiply_fusion), calls=%async_computation | async-start | bytes 6291456 | tf_op jit(solution)/shard_map/all_to_all | solution.py:114
  108.3 2.6 %iota_compare_fusion = pred[576,3072]{1,0:T(8,128)(4,1)} fusion(s32[576]{0:T(1024)S(1)} %reduce.4), kind=kLoop, calls=%fused_computation.11 | loop fusion | flops 1769472 | bytes 1771776 | tf_op jit(solution)/shard_map/le | solution.py:127
  110.9 1.5 convert_reduce_fusion
  112.6 6.8 %collective-permute-done = bf16[576,64]{0,1:T(8,128)(2,1)S(1)} collective-permute-done((bf16[576,64]{0,1:T(8,128)(2,1)S(1)}, bf16[576,64]{0,1:T(8,128)(2,1)S(1)}, u32[]{:S(2)}, u32[]{:S(2)}) %collective-permute-start) | collective-permute-done | bytes 73760 | tf_op jit(solution)/shard_map/ppermute | solution.py:33
  120.2 14.4 %collective-permute-done.1 = bf16[576,128]{0,1:T(8,128)(2,1)} collective-permute-done((bf16[576,128]{0,1:T(8,128)(2,1)}, bf16[576,128]{0,1:T(8,128)(2,1)}, u32[]{:S(2)}, u32[]{:S(2)}) %collective-permute-start.1) | collective-permute-done | bytes 147488 | tf_op jit(solution)/shard_map/ppermute | solution.py:33
  134.6 1.7 convert_element_type.95
  136.2 9.9 %all-to-all-done = bf16[16,384,256]{2,1,0:T(8,128)(2,1)S(1)} async-done(((bf16[16,384,256]{2,1,0:T(8,128)(2,1)}), bf16[16,384,256]{2,1,0:T(8,128)(2,1)S(1)}, u32[]{:S(2)}, u32[]{:S(2)}) %all-to-all-start) | async-done | bytes 3145760 | tf_op jit(solution)/shard_map/all_to_all | solution.py:114
  146.1 1.8 gather_fusion.1
  148.0 1.6 broadcast_select_fusion
  149.6 1.1 fusion.31
  151.8 25.4 %all-gather.7.cloned.1.call-done = bf16[16,576,512]{2,1,0:T(8,128)(2,1)} async-done(((bf16[2,576,512]{2,1,0:T(8,128)(2,1)}), bf16[16,576,512]{2,1,0:T(8,128)(2,1)}) %all-gather.7.cloned.1.call-update) | async-done | bytes 9437200 | tf_op jit(solution)/shard_map/all_gather | solution.py:45
  177.2 8.2 %copy.40 = bf16[2,8,1,576,512]{4,3,1,0,2:T(8,128)(2,1)} copy(bf16[2,8,1,576,512]{4,3,0,1,2:T(8,128)(2,1)} %bitcast.70) | data formatting | bytes 18874368 | tf_op jit(solution)/shard_map/transpose | solution.py:49
  185.4 5.7 %multiply_reduce_fusion = f32[576]{0:T(1024)S(1)} fusion(bf16[1,576,16,512]{3,1,2,0:T(8,128)(2,1)} %bitcast.68), kind=kLoop, calls=%fused_computation.5 | loop fusion | flops 14155200 | bytes 9439488 | tf_op jit(solution)/shard_map/reduce_sum | solution.py:93
  191.8 1.3 subtract_convert_fusion.1
  194.2 8.7 %copy.53 = bf16[72,8,16,512]{3,1,2,0:T(8,128)(2,1)} copy(bf16[72,8,16,512]{3,1,0,2:T(8,128)(2,1)} %bitcast.69) | data formatting | bytes 18874368
  202.9 10.7 %convolution_multiply_fusion = f32[576,256]{0,1:T(8,128)S(1)} fusion(bf16[576,8192]{1,0:T(8,128)(2,1)} %bitcast.71, bf16[8192,256]{1,0:T(8,128)(2,1)} %param.8, f32[576]{0:T(1024)S(1)} %add_rsqrt_fusion), kind=kOutput, calls=%fused_computation.21 | convolution fusion | flops 2416066560 | bytes 14223616 | tf_op jit(solution)/shard_map/dot_general | solution.py:92
  214.1 1.6 pad_maximum_fusion.1
  215.7 1.7 copy.42
  217.3 1.7 copy.41
  219.0 5.0 %scatter_fusion.1 = bf16[3072,128]{1,0:T(8,128)(2,1)S(1)} fusion(bf16[3072,128]{1,0:T(8,128)(2,1)S(1)} %pad_maximum_fusion, s32[576]{0:T(1024)S(1)} %fusion.25, bf16[576,128]{1,0:T(8,128)(2,1)} %copy.42), kind=kCustom, calls=%fused_computation.3 | custom fusion | bytes 444672 | tf_op jit(solution)/shard_map/scatter | solution.py:125
  224.1 5.3 %scatter_fusion = bf16[3072,128]{1,0:T(8,128)(2,1)S(1)} fusion(bf16[3072,128]{1,0:T(8,128)(2,1)S(1)} %bitcast.73, s32[576]{0:T(1024)S(1)} %fusion.25, bf16[576,128]{1,0:T(8,128)(2,1)} %copy.41), kind=kCustom, calls=%fused_computation.2 | custom fusion | bytes 444672 | tf_op jit(solution)/shard_map/scatter | solution.py:126
  229.4 1.3 multiply_subtract_fusion
  230.6 12.1 %fusion.33 = (f32[2,576]{1,0:T(2,128)S(1)}, f32[2,576,3072]{2,1,0:T(8,128)}) fusion(pred[576,3072]{1,0:T(8,128)(4,1)} %iota_compare_fusion, bf16[3072,128]{1,0:T(8,128)(2,1)S(1)} %scatter_fusion.1, f32[576,2,64]{2,0,1:T(8,128)} %get-tuple-element.11, f32[576,2,64]{2,0,1:T(8,128)} %get-tuple-element.10), kind=kOutput, calls=%fused_computation.82 | convolution fusion | flops 917031936 | bytes 17306112 | tf_op jit(solution)/shard_map/sub | solution.py:131
  242.7 7.5 %fusion.9 = bf16[576,2,128]{2,0,1:T(8,128)(2,1)S(1)} fusion(f32[2,576,3072]{2,1,0:T(8,128)} %get-tuple-element.25, f32[2,576]{1,0:T(2,128)S(1)} %get-tuple-element.24, bf16[3072,128]{1,0:T(8,128)(2,1)} %copy-done.3, pred[576]{0:T(1024)(128)(4,1)S(1)} %iota_compare_fusion.1), kind=kOutput, calls=%fused_computation.24 | convolution fusion | flops 913342464 | bytes 15242304 | tf_op jit(solution)/shard_map/grs,sd->rgd/dot_general | solution.py:133
  (54 shorter events, 6.6 us)
Async XLA Ops:
  6.5 46.4 %copy-start = (bf16[4,4,384,256]{3,2,1,0:T(8,128)(2,1)S(1)}, bf16[4,4,384,256]{3,2,1,0:T(8,128)(2,1)}, u32[]{:S(2)}) copy-start(bf16[4,4,384,256]{3,2,1,0:T(8,128)(2,1)} %param.10) | copy-start | bytes 9437188
  6.5 33.4 %all-gather.5.cloned.1.call-start = ((), (), s32[]{:S(2)}) async-start(), calls=%async_computation.2 | async-start | bytes 1769472 | tf_op jit(solution)/shard_map/all_gather | solution.py:45
  7.3 169.9 %all-gather.7.cloned.1.call-start = ((), (), s32[]{:S(2)}) async-start(), calls=%async_computation.3 | async-start | bytes 10616832 | tf_op jit(solution)/shard_map/all_gather | solution.py:45
  43.2 9.6 %copy-start.6 = (s32[16,8]{0,1:T(8,128)S(1)}, s32[16,8]{0,1:T(8,128)}, u32[]{:S(2)}) copy-start(s32[16,8]{0,1:T(8,128)} %param.11) | copy-start | bytes 1540
  45.6 54.5 %all-to-all-start.1 = ((bf16[16,576,64]{1,2,0:T(8,128)(2,1)}), bf16[16,576,64]{1,2,0:T(8,128)(2,1)}, u32[]{:S(2)}, u32[]{:S(2)}) async-start(bf16[16,576,64]{1,2,0:T(8,128)(2,1)} %bitcast.72), calls=%async_computation.1 | async-start | bytes 2621440 | tf_op jit(solution)/shard_map/all_to_all | solution.py:28
  57.8 49.5 %copy-start.7 = (s32[1,576]{1,0:T(1,128)S(1)}, s32[1,576]{1,0:T(1,128)}, u32[]{:S(2)}) copy-start(s32[1,576]{1,0:T(1,128)} %param.12) | copy-start | bytes 6916
  100.1 46.1 %all-to-all-start = ((bf16[16,384,256]{2,1,0:T(8,128)(2,1)}), bf16[16,384,256]{2,1,0:T(8,128)(2,1)S(1)}, u32[]{:S(2)}, u32[]{:S(2)}) async-start(bf16[16,384,256]{2,1,0:T(8,128)(2,1)} %select_multiply_fusion), calls=%async_computation | async-start | bytes 6291456 | tf_op jit(solution)/shard_map/all_to_all | solution.py:114
  112.5 6.9 %collective-permute-start = (bf16[576,64]{0,1:T(8,128)(2,1)S(1)}, bf16[576,64]{0,1:T(8,128)(2,1)S(1)}, u32[]{:S(2)}, u32[]{:S(2)}) collective-permute-start(bf16[576,64]{0,1:T(8,128)(2,1)S(1)} %convert_element_type.92), channel_id=1, source_target_pairs={{0,1},{1,0},{2,3},{3,2},{4,5},{5,4},{6,7},{7,6},{8,9},{9,8},{10,11... | collective-permute-start | bytes 221192 | tf_op jit(solution)/shard_map/ppermute | solution.py:33
  120.1 14.5 %collective-permute-start.1 = (bf16[576,128]{0,1:T(8,128)(2,1)}, bf16[576,128]{0,1:T(8,128)(2,1)}, u32[]{:S(2)}, u32[]{:S(2)}) collective-permute-start(bf16[576,128]{0,1:T(8,128)(2,1)} %get-tuple-element.5), channel_id=1, source_target_pairs={{0,2},{1,3},{2,0},{3,1},{4,6},{5,7},{6,4},{7,5},{8,10},{9,11},{10,... | collective-permute-start | bytes 442376 | tf_op jit(solution)/shard_map/ppermute | solution.py:33
  185.4 5.7 %copy-start.4 = (f32[576,128]{0,1:T(8,128)S(1)}, f32[576,128]{0,1:T(8,128)}, u32[]{:S(2)}) copy-start(f32[576,128]{0,1:T(8,128)} %convert_element_type.95) | copy-start | bytes 884740
  213.5 10.5 %copy-start.2 = (bf16[8,384,128]{2,1,0:T(8,128)(2,1)S(1)}, bf16[8,384,128]{2,1,0:T(8,128)(2,1)}, u32[]{:S(2)}) copy-start(bf16[8,384,128]{2,1,0:T(8,128)(2,1)} %get-tuple-element.14) | copy-start | bytes 2359300
  214.0 15.3 %copy-start.5 = (f32[576,64]{1,0:T(8,128)S(1)}, f32[576,64]{1,0:T(8,128)}, u32[]{:S(2)}) copy-start(f32[576,64]{1,0:T(8,128)} %copy.48) | copy-start | bytes 442372
  229.4 13.3 %copy-start.3 = (bf16[3072,128]{1,0:T(8,128)(2,1)}, bf16[3072,128]{1,0:T(8,128)(2,1)S(1)}, u32[]{:S(2)}) copy-start(bf16[3072,128]{1,0:T(8,128)(2,1)S(1)} %scatter_fusion) | copy-start | bytes 2359300
  242.7 8.7 %copy-start.1 = (bf16[4,4,384,256]{3,2,1,0:T(8,128)(2,1)S(1)}, bf16[4,4,384,256]{3,2,1,0:T(8,128)(2,1)}, u32[]{:S(2)}) copy-start(bf16[4,4,384,256]{3,2,1,0:T(8,128)(2,1)} %param.10) | copy-start | bytes 9437188
Sparse Core Ops, SparseCore 0:
  9.1 30.7 all-gather.4
  41.7 135.4 all-gather.6
where the time goes:
time: 260 us; the launch traced here: 258 us
  waiting for transfers between devices  132 us (51%)
  local copies, waits for them, and re-layouts  41.3 us (16%)
  matrix products  33.4 us (13%)
  other arithmetic  22.5 us (9%)
  starting transfers between devices  14.5 us (6%)
  between operations  14.4 us (6%)
    all_gather x2, waiting for transfers between devices, stacked_from(): parts = lax.all_gather(parts, axes[k], axis=0, tiled=True)  58.1 us
    all_to_all x1, waiting for transfers between devices, summed_on_arrival(): lax.all_to_all(parts, axis, split_axis=0, concat_axis=0, tiled=True)  42.2 us
    ppermute x2, waiting for transfers between devices, from_partner(): lax.ppermute(value, axis, [(i, i ^ 1 << bit) for i in range(lax.axis_size...  21.2 us
    sub x1, matrix products, local(): shifted = jnp.exp(scores - row_max)  12.1 us
    dot_general x1, matrix products, local(): running = jnp.dot(token_part, w_query, preferred_element_type=jnp.float32)  10.7 us
    all_to_all x1, waiting for transfers between devices, local(): lax.all_to_all(outgoing, 'store', split_axis=0, concat_axis=0, tiled=True)  9.9 us
    unnamed x19, local copies, waits for them, and re-layouts  9.17 us
    transpose x1, local copies, waits for them, and re-layouts, stacked_from(): parts.transpose(*turned, *range(len(sequence), parts.ndim))  8.17 us
  transfers between devices with their start and end apart: 6, of which 6 were waited for; matrix products, arithmetic and copies ran while one was open for 9% of the time, Pallas kernels for 0%

commit v1 on v0

v1 whole, which is shorter than its diff:
```python
import functools
import math

import jax
import jax.numpy as jnp
from jax import lax
from jax.experimental import pallas as pl
from jax.experimental.pallas import tpu as pltpu
from jax.sharding import PartitionSpec as P

D = 8192
KV_HEADS = 4
HEAD_DIM = 128
PASSAGE = 384
PASSAGES = 8
SEQ = 3072
ROWS = 576
ROPE_BASE = 1000000.0
EPSILON = 1e-06
BLOCK = 144
NEG = -1e30
FAR = 1 << 20


def turned(vectors, cosine, sine):
    return vectors * cosine + pltpu.roll(vectors, HEAD_DIM // 2, 1) * sine


def turn_tables(positions):
    half = HEAD_DIM // 2
    frequency = ROPE_BASE ** (-(jnp.arange(half, dtype=jnp.float32) * 2.0) / HEAD_DIM)
    angles = positions.astype(jnp.float32)[..., None] * frequency
    cosine, sine = jnp.cos(angles), jnp.sin(angles)
    return jnp.concatenate([cosine, cosine, -sine, sine], axis=-1)


def attend_kernel(
    ids_sm, pos_sm, count_sm, q_ref, kv_ref, inv_ref, pos_ref, table_ref, old_table_ref,
    incoming_ref, out_ref, q_s, nk_s, nv_s, kk_s, vv_s, kp_s, acc_s,
):
    heads = q_ref.shape[1] // HEAD_DIM
    count = count_sm[0]
    inverse = inv_ref[:ROWS, :1]
    store = lax.axis_index("store")
    cosine, sine = table_ref[:, :HEAD_DIM], table_ref[:, HEAD_DIM:]
    scale = HEAD_DIM**-0.5 * math.log2(math.e)
    for h in range(heads):
        part = q_ref[:, h * HEAD_DIM : (h + 1) * HEAD_DIM].astype(jnp.float32) * inverse
        q_s[h] = (turned(part, cosine, sine) * scale).astype(jnp.bfloat16)
    fresh = kv_ref[:, :HEAD_DIM].astype(jnp.float32) * inverse
    nk_s[:ROWS] = turned(fresh, cosine, sine).astype(jnp.bfloat16)
    nk_s[ROWS:] = jnp.zeros_like(nk_s[ROWS:])
    nv_s[:ROWS, :HEAD_DIM] = (kv_ref[:, HEAD_DIM:].astype(jnp.float32) * inverse).astype(jnp.bfloat16)
    nv_s[ROWS:, :HEAD_DIM] = jnp.zeros_like(nv_s[ROWS:, :HEAD_DIM])
    nv_s[:, HEAD_DIM:] = jnp.ones_like(nv_s[:, HEAD_DIM:])
    row_ids = lax.broadcasted_iota(jnp.int32, (ROWS, 1), 0)
    marked = jnp.where(row_ids < count, pos_ref[...], -1)

    def prepare(k, carry):
        block = incoming_ref[ids_sm[store, k] // 4]
        table = old_table_ref[k]
        keys = block[:, :HEAD_DIM].astype(jnp.float32)
        kk_s[k] = turned(keys, table[:, :HEAD_DIM], table[:, HEAD_DIM:]).astype(jnp.bfloat16)
        vv_s[k, :, :HEAD_DIM] = block[:, HEAD_DIM:]
        vv_s[k, :, HEAD_DIM:] = jnp.ones_like(block[:, HEAD_DIM:])
        here = k * PASSAGE + lax.broadcasted_iota(jnp.int32, (1, PASSAGE), 1)
        hit = jnp.max(jnp.where(marked == here, FAR, 0), axis=0, keepdims=True)
        kp_s[k] = jnp.broadcast_to(jnp.maximum(here, hit), (8, PASSAGE))
        return carry

    lax.fori_loop(0, PASSAGES, prepare, 0)
    contract = (((1,), (1,)), ((), ()))
    for b in range(ROWS // BLOCK):
        low, high = b * BLOCK, (b + 1) * BLOCK
        rows = heads * BLOCK

        @pl.when(low >= count)
        def _():
            out_ref[low:high] = jnp.zeros_like(out_ref[low:high])

        @pl.when(low < count)
        def _():
            queries = q_s[:, low:high].reshape(rows, HEAD_DIM)
            width = -(-high // 128) * 128
            scores = lax.dot_general(
                queries, nk_s[:width], contract, preferred_element_type=jnp.float32
            )
            row_of = low + lax.broadcasted_iota(jnp.int32, (BLOCK, width), 0)
            key_of = lax.broadcasted_iota(jnp.int32, (BLOCK, width), 1)
            seen = jnp.concatenate([key_of <= row_of] * heads, axis=0)
            scores = jnp.where(seen, scores, NEG)
            top = jnp.max(scores, axis=1, keepdims=True)
            weight = jnp.exp2(scores - top).astype(jnp.bfloat16)
            acc_s[...] = jnp.dot(weight, nv_s[:width], preferred_element_type=jnp.float32)
            place = pos_ref[low:high]
            place = jnp.concatenate([place] * heads, axis=0)
            last = jnp.minimum(count, high) - 1

            def old(k, top):
                scores = lax.dot_general(
                    queries, kk_s[k], contract, preferred_element_type=jnp.float32
                )
                scores = jnp.where(kp_s[k, 0:1] <= place, scores, NEG)
                risen = jnp.maximum(top, jnp.max(scores, axis=1, keepdims=True))
                weight = jnp.exp2(scores - risen).astype(jnp.bfloat16)
                part = jnp.dot(weight, vv_s[k], preferred_element_type=jnp.float32)
                acc_s[...] = acc_s[...] * jnp.exp2(top - risen) + part
                return risen

            lax.fori_loop(0, pos_sm[0, last] // PASSAGE + 1, old, top)
            result = acc_s[:, :HEAD_DIM] / acc_s[:, HEAD_DIM:]
            live = low + lax.broadcasted_iota(jnp.int32, (BLOCK, HEAD_DIM), 0) < count
            for h in range(heads):
                piece = jnp.where(live, result[h * BLOCK : (h + 1) * BLOCK], 0.0)
                out_ref[low:high, h * HEAD_DIM : (h + 1) * HEAD_DIM] = piece.astype(jnp.bfloat16)


def attend(passage_ids, select_index, select_count, q_raw, kv_raw, inverse, table, incoming):
    heads = q_raw.shape[1] // HEAD_DIM
    old_table = turn_tables(jnp.arange(PASSAGES) * PASSAGE)[:, None]
    smem = pl.BlockSpec(memory_space=pltpu.SMEM)
    vmem = pl.BlockSpec(memory_space=pltpu.VMEM)
    return pl.pallas_call(
        attend_kernel,
        out_shape=jax.ShapeDtypeStruct((ROWS, q_raw.shape[1]), jnp.bfloat16),
        in_specs=[smem] * 3 + [vmem] * 7,
        out_specs=vmem,
        scratch_shapes=[
            pltpu.VMEM((heads, ROWS, HEAD_DIM), jnp.bfloat16),
            pltpu.VMEM((640, HEAD_DIM), jnp.bfloat16),
            pltpu.VMEM((640, 2 * HEAD_DIM), jnp.bfloat16),
            pltpu.VMEM((PASSAGES, PASSAGE, HEAD_DIM), jnp.bfloat16),
            pltpu.VMEM((PASSAGES, PASSAGE, 2 * HEAD_DIM), jnp.bfloat16),
            pltpu.VMEM((PASSAGES, 8, PASSAGE), jnp.int32),
            pltpu.VMEM((heads * BLOCK, 2 * HEAD_DIM), jnp.float32),
        ],
        name="attend",
        cost_estimate=pl.CostEstimate(flops=2 * 10**9, bytes_accessed=5 * 10**6, transcendentals=0),
        compiler_params=pltpu.CompilerParams(vmem_limit_bytes=40 << 20),
    )(passage_ids, select_index, select_count, q_raw, kv_raw, inverse, select_index.reshape(ROWS, 1),
      table, old_table, incoming)


RELS = (1, 7, 2, 6, 3, 5, 4)
GROUPS = ((0, 2), (2, 2), (4, 3))
KV_PARTS = ((0, 48), (48, 32), (80, 32), (112, 32))
FLOWS = 4
SHARE = ROWS // FLOWS
STEPS = 7
MESH = pl.DeviceIdType.MESH


def exchange_kernel(
    ids_sm, pos_ref, hidden_ref, query_ref, keyvalue_ref, cache_ref,
    q_ref, kv_ref, inv_ref, table_ref, incoming_ref,
    held, weights, kv_weights, pool, outgoing, sending, arriving, partial, squares, fresh,
    local_sem, h_send, h_recv, z_send, z_recv, k_send, k_recv, kd_send, kd_recv,
    x_send, x_recv, f_send, f_recv, d_send, d_recv, r_send, r_recv,
    s_send, s_recv, g_send, g_recv, p_send, p_recv,
):
    store = lax.axis_index("store")
    rank = lax.axis_index("tp")
    x, high, core = store // 4, (store // 2) % 2, store % 2
    low, z = rank // 8, rank % 8
    quarter = z % 4
    head = rank // 4

    def place(to_x=x, to_core=core, to_low=low, to_z=z):
        return (to_x * 4 + high * 2 + to_core, to_low * 8 + to_z)

    def remote(source, target, send, recv, device):
        return pltpu.make_async_remote_copy(
            src_ref=source, dst_ref=target, send_sem=send, recv_sem=recv,
            device_id=device, device_id_type=MESH,
        )

    def piece(owner):
        return pl.ds(pl.multiple_of(owner * 64, 64), 64)

    locals_ = [
        pltpu.make_async_copy(hidden_ref, held.at[low], local_sem.at[0]),
        pltpu.make_async_copy(cache_ref.at[:, head], pool, local_sem.at[1]),
        pltpu.make_async_copy(query_ref.at[:, z], weights.at[7], local_sem.at[2]),
    ]
    for h in range(2):
        columns = pl.ds(pl.multiple_of((low * 2 + h) * 256, 256), 256)
        locals_.append(
            pltpu.make_async_copy(
                keyvalue_ref.at[:, columns], kv_weights.at[low, h], local_sem.at[3 + h]
            )
        )
    for copy in locals_:
        copy.start()

    barrier = pltpu.get_barrier_semaphore()
    for d in range(1, 16):
        pl.semaphore_signal(
            barrier, inc=1, device_id=((store + d) % 16, rank), device_id_type=MESH
        )
    for d in range(1, 8):
        pl.semaphore_signal(
            barrier, inc=1, device_id=place(to_z=(z + d) % 8), device_id_type=MESH
        )
    pl.semaphore_signal(barrier, inc=1, device_id=place(to_low=1 - low), device_id_type=MESH)
    pl.semaphore_wait(barrier, 23)

    across = place(to_low=1 - low)
    rows_of = [remote(
        hidden_ref.at[pl.ds(f * SHARE, SHARE)], held.at[low, pl.ds(f * SHARE, SHARE)],
        h_send.at[f], h_recv.at[f], across,
    ) for f in range(FLOWS)]
    mine = piece(x * 2 + core)
    spread = [remote(
        query_ref.at[:, (z + 8 - rel) % 8, mine], weights.at[o, :, mine],
        z_send.at[o], z_recv.at[o], place(to_z=(z + 8 - rel) % 8),
    ) for o, rel in enumerate(RELS)]
    half = pl.ds(pl.multiple_of(core * 256, 256), 256)
    kv_rows = []
    kv_shared = []
    for h in range(2):
        columns = pl.ds(pl.multiple_of(((1 - low) * 2 + h) * 256, 256), 256)
        kv_rows.append(remote(
            keyvalue_ref.at[half, columns], kv_weights.at[low, h, half],
            k_send.at[h], k_recv.at[h], across,
        ))
        kv_shared.append(remote(
            kv_weights.at[1 - low, h, half], kv_weights.at[1 - low, h, half],
            kd_send.at[h], kd_recv.at[h], place(to_core=1 - core),
        ))
    for copy in spread[:2] + rows_of + spread[2:] + kv_rows:
        copy.start()

    turn = 1 - 2 * core
    owners = (x, (x + 3) % 4, (x + 1) % 4, (x + 2) % 4)

    def group(g, owner):
        start, size = GROUPS[g]
        return weights.at[pl.ds(start, size), :, piece(owner * 2 + core)]

    def beside(g, way):
        to = (x + 1) % 4 if way == 0 else (x + 3) % 4
        return remote(
            group(g, x), group(g, x), x_send.at[g, way], x_recv.at[g, way], place(to_x=to)
        )

    def onward(g):
        owner = (x + 4 - turn) % 4
        to = (x + 4 + turn) % 4
        return remote(group(g, owner), group(g, owner), f_send.at[g], f_recv.at[g], place(to_x=to))

    def twin(g, i):
        block = group(g, owners[i])
        return remote(block, block, d_send.at[g, i], d_recv.at[g, i], place(to_core=1 - core))

    def first(g):
        start, size = GROUPS[g]
        for o in range(start, start + size):
            spread[o].wait_recv()
        beside(g, 0).start()
        beside(g, 1).start()
        twin(g, 0).start()

    def second(g):
        beside(g, 0).wait_recv()
        beside(g, 1).wait_recv()
        onward(g).start()
        twin(g, 1).start()
        twin(g, 2).start()

    def third(g):
        onward(g).wait_recv()
        twin(g, 3).start()

    def fourth(g):
        for i in range(4):
            twin(g, i).wait_recv()

    locals_[1].wait()

    def choose(d, carry):
        to = (store + d) % 16
        slot = jnp.int32(0)
        for k in range(PASSAGES):
            entry = ids_sm[to, k]
            slot = slot + jnp.where(entry // 4 == store, entry % 4, 0)
        outgoing[d] = pool[slot]
        return carry

    lax.fori_loop(0, 16, choose, 0)
    keep = pltpu.make_async_copy(outgoing.at[0], incoming_ref.at[store], local_sem.at[5])
    keep.start()
    passages = [remote(
        outgoing.at[d], incoming_ref.at[store], p_send.at[d - 1], p_recv.at[d - 1],
        ((store + d) % 16, rank),
    ) for d in range(1, 16)]

    first(0)
    first(1)
    second(0)
    first(2)
    third(0)
    second(1)
    third(1)
    second(2)
    for copy in passages:
        copy.start()
    for h in range(2):
        kv_rows[h].wait_recv()
        kv_shared[h].start()
    half_dim = HEAD_DIM // 2
    lane = lax.broadcasted_iota(jnp.int32, (1, HEAD_DIM), 1) % half_dim
    frequency = jnp.exp(lane.astype(jnp.float32) * (-2.0 * math.log(ROPE_BASE) / HEAD_DIM))
    angles = pos_ref[...].astype(jnp.float32) * frequency
    table_ref[:, :HEAD_DIM] = jnp.cos(angles)
    side = jnp.where(lax.broadcasted_iota(jnp.int32, (1, HEAD_DIM), 1) < half_dim, -1.0, 1.0)
    table_ref[:, HEAD_DIM:] = jnp.sin(angles) * side

    locals_[0].wait()
    locals_[2].wait()
    locals_[3].wait()
    locals_[4].wait()
    third(2)
    for h in range(2):
        kv_shared[h].wait_recv()
    fourth(0)
    fourth(1)
    fourth(2)

    def slot_of(f, s):
        if f % 2 == 0:
            return jnp.where(s < 3, 2 * s + 1, jnp.where(s == STEPS, 7, 12 - 2 * s))
        return jnp.where(s <= 3, 2 * s, jnp.where(s == STEPS, 7, 13 - 2 * s))

    def target_of(f, s):
        return (z + 15 - s) % 8 if f % 2 == 0 else (z + 1 + s) % 8

    def add_up(f, s):
        slot, to = slot_of(f, s), target_of(f, s)
        rows = pl.ds(f * SHARE, SHARE)
        offset, size = KV_PARTS[f]
        kv_rows_of = pl.ds(pl.multiple_of((to % 4) * SHARE + offset, 16), size)
        total = jnp.zeros((SHARE, 256), jnp.float32)
        kv_total = jnp.zeros((size, 256), jnp.float32)
        for b in range(2):
            total += jnp.dot(held[b, rows], weights[slot, b], preferred_element_type=jnp.float32)
            kv_total += jnp.dot(
                held[b, kv_rows_of], kv_weights[b, to // 4], preferred_element_type=jnp.float32
            )
        partial[f, :SHARE] = total
        partial[f, SHARE : SHARE + size] = kv_total

    def hop(f, s):
        to = (z + 1) % 8 if f % 2 == 0 else (z + 7) % 8
        size = SHARE + KV_PARTS[f][1]
        return remote(
            sending.at[f, s, pl.ds(0, size)], arriving.at[f, s, pl.ds(0, size)],
            r_send.at[f, s], r_recv.at[f, s], place(to_z=to),
        )

    for f in range(FLOWS):
        rows_of[f].wait_recv()
    for f in range(FLOWS):
        size = SHARE + KV_PARTS[f][1]
        add_up(f, 0)
        sending[f, 0, :size] = partial[f, :size].astype(jnp.bfloat16)
        hop(f, 0).start()

    ones = jnp.ones((8, 512), jnp.bfloat16)
    along = (((1,), (1,)), ((), ()))
    sum_of = jnp.zeros((8, ROWS), jnp.float32)
    for b in range(2):
        wide = held[b].astype(jnp.float32)
        square = wide * wide
        upper = square.astype(jnp.bfloat16)
        lower = (square - upper.astype(jnp.float32)).astype(jnp.bfloat16)
        sum_of += lax.dot_general(ones, upper, along, preferred_element_type=jnp.float32)
        sum_of += lax.dot_general(ones, lower, along, preferred_element_type=jnp.float32)
    squares[z, :, :ROWS] = sum_of
    squares[z, :, ROWS:] = jnp.zeros((8, 640 - ROWS), jnp.float32)
    sums = [remote(
        squares.at[z], squares.at[z], s_send.at[d - 1], s_recv.at[d - 1],
        place(to_z=(z + d) % 8),
    ) for d in range(1, 8)]
    for copy in sums:
        copy.start()

    def step(s, carry):
        for f in range(FLOWS):
            size = SHARE + KV_PARTS[f][1]
            add_up(f, s)
            hop(f, s - 1).wait_recv()
            total = partial[f, :size] + arriving[f, s - 1, :size].astype(jnp.float32)
            sending[f, s, :size] = total.astype(jnp.bfloat16)
            hop(f, s).start()
        return carry

    lax.fori_loop(1, STEPS, step, 0)
    for f in range(FLOWS):
        offset, size = KV_PARTS[f]
        add_up(f, jnp.int32(STEPS))
        hop(f, STEPS - 1).wait_recv()
        got = arriving[f, STEPS - 1].astype(jnp.float32)
        q_ref[f * SHARE : (f + 1) * SHARE] = partial[f, :SHARE] + got[:SHARE]
        kv_total = partial[f, SHARE : SHARE + size] + got[SHARE : SHARE + size]
        fresh[quarter, offset : offset + size] = kv_total.astype(jnp.bfloat16)
    shared = [remote(
        fresh.at[quarter], fresh.at[quarter], g_send.at[d - 1], g_recv.at[d - 1],
        place(to_z=(z // 4) * 4 + (quarter + d) % 4),
    ) for d in range(1, 4)]
    for copy in shared:
        copy.start()
    for copy in sums:
        copy.wait_recv()
    total = squares[0]
    for b in range(1, 8):
        total += squares[b]
    inv_ref[...] = jnp.transpose(lax.rsqrt(total * (1.0 / D) + EPSILON))
    for copy in shared:
        copy.wait_recv()
    for i in range(4):
        kv_ref[i * SHARE : (i + 1) * SHARE] = fresh[i]
    for copy in passages:
        copy.wait_recv()
    keep.wait()
    for copy in rows_of + spread + kv_rows + kv_shared + passages + sums + shared:
        copy.wait_send()
    for g in range(3):
        beside(g, 0).wait_send()
        beside(g, 1).wait_send()
        onward(g).wait_send()
        for i in range(4):
            twin(g, i).wait_send()

    def drained(s, carry):
        for f in range(FLOWS):
            hop(f, s).wait_send()
        return carry

    lax.fori_loop(0, STEPS, drained, 0)


def exchange(passage_ids, select_index, hidden, w_query, w_keyvalue, passage_cache):
    smem = pl.BlockSpec(memory_space=pltpu.SMEM)
    vmem = pl.BlockSpec(memory_space=pltpu.VMEM)
    hbm = pl.BlockSpec(memory_space=pl.ANY)
    dma = pltpu.SemaphoreType.DMA
    return pl.pallas_call(
        exchange_kernel,
        out_shape=(
            jax.ShapeDtypeStruct((ROWS, 256), jnp.float32),
            jax.ShapeDtypeStruct((ROWS, 256), jnp.bfloat16),
            jax.ShapeDtypeStruct((640, 8), jnp.float32),
            jax.ShapeDtypeStruct((ROWS, 2 * HEAD_DIM), jnp.float32),
            jax.ShapeDtypeStruct((16, PASSAGE, 256), jnp.bfloat16),
        ),
        in_specs=[smem, vmem, hbm, hbm, hbm, hbm],
        out_specs=(vmem, vmem, vmem, vmem, hbm),
        scratch_shapes=[
            pltpu.VMEM((2, ROWS, 512), jnp.bfloat16),
            pltpu.VMEM((8, 2, 512, 256), jnp.bfloat16),
            pltpu.VMEM((2, 2, 512, 256), jnp.bfloat16),
            pltpu.VMEM((4, PASSAGE, 256), jnp.bfloat16),
            pltpu.VMEM((16, PASSAGE, 256), jnp.bfloat16),
            pltpu.VMEM((FLOWS, STEPS, 192, 256), jnp.bfloat16),
            pltpu.VMEM((FLOWS, STEPS, 192, 256), jnp.bfloat16),
            pltpu.VMEM((FLOWS, 192, 256), jnp.float32),
            pltpu.VMEM((8, 8, 640), jnp.float32),
            pltpu.VMEM((4, SHARE, 256), jnp.bfloat16),
            dma((6,)), dma((4,)), dma((4,)), dma((7,)), dma((7,)), dma((2,)), dma((2,)),
            dma((2,)), dma((2,)), dma((3, 2)), dma((3, 2)), dma((3,)), dma((3,)),
            dma((3, 4)), dma((3, 4)), dma((4, 7)), dma((4, 7)), dma((7,)), dma((7,)),
            dma((3,)), dma((3,)), dma((15,)), dma((15,)),
        ],
        name="exchange",
        cost_estimate=pl.CostEstimate(
            flops=3 * 10**9, bytes_accessed=10**7, transcendentals=0
        ),
        compiler_params=pltpu.CompilerParams(
            collective_id=0, has_side_effects=True, vmem_limit_bytes=56 << 20
        ),
    )(
        passage_ids,
        select_index.reshape(ROWS, 1),
        hidden.reshape(ROWS, 512),
        w_query.reshape(2, 8, 512, 256),
        w_keyvalue,
        passage_cache,
    )


def local(hidden, w_query, w_keyvalue, passage_cache, passage_ids, select_index, select_count):
    q_raw, kv_raw, inverse, table, incoming = exchange(
        passage_ids, select_index, hidden, w_query, w_keyvalue, passage_cache
    )
    context = attend(
        passage_ids, select_index, select_count, q_raw, kv_raw, inverse, table, incoming
    )
    return context[None]


def solution(mesh):
    placed = (
        P("store", None, "tp"),
        P(None, "tp"),
        P("tp", None),
        P("store", None, None, None),
        P(),
        P("store", None),
        P("store"),
    )
    return jax.shard_map(
        local, mesh=mesh, in_specs=placed, out_specs=P("store", None, "tp"), check_vma=False
    )
```

time: 260 us -> 127 us (0.49)
  waiting for transfers between devices: 132 us -> 0 us
  Pallas kernels: 0 us -> 117 us
  matrix products: 33.4 us -> 0 us
  local copies, waits for them, and re-layouts: 41.3 us -> 8.88 us
  other arithmetic: 22.5 us -> 0.2 us
  starting transfers between devices: 14.5 us -> 0 us
  between operations: 14.4 us -> 0.71 us
    pallas_call x0 -> x2, Pallas kernels: none -> 117 us  [the longest x1 98.4 us: exchange(): pl.pallas_call(exchange_kernel, out_shape=(jax.ShapeDtypeStruct((ROWS, 25...]
    all_gather x2 -> x0, waiting for transfers between devices: 58.1 us -> none  [stacked_from(): parts = lax.all_gather(parts, axes[k], axis=0, tiled=True)]
    all_to_all x2 -> x0, waiting for transfers between devices: 52.1 us -> none  [the longest x1 42.2 us: summed_on_arrival(): lax.all_to_all(parts, axis, split_axis=0, concat_axis=0, tiled=True)]
    dot_general x3 -> x0, matrix products: 21.3 us -> none  [the longest x1 10.7 us: local(): running = jnp.dot(token_part, w_query, preferred_element_type=jnp.float32)]
    ppermute x2 -> x0, waiting for transfers between devices: 21.2 us -> none  [from_partner(): lax.ppermute(value, axis, [(i, i ^ 1 << bit) for i in range(lax.axis_size...]
    all_to_all x2 -> x0, starting transfers between devices: 14.4 us -> none  [the longest x1 7.25 us: local(): lax.all_to_all(outgoing, 'store', split_axis=0, concat_axis=0, tiled=True)]
    sub x1 -> x0, matrix products: 12.1 us -> none  [local(): shifted = jnp.exp(scores - row_max)]
    scatter x2 -> x0, local copies, waits for them, and re-layouts: 10.3 us -> none  [the longest x1 5.27 us: local(): all_values = old_values.at[target].set(new_values, mode='drop')]
  transfers between devices with their start and end apart: 6 -> 0, of which waited for: 6 -> 0; matrix products, arithmetic and copies ran while one was open for 9% -> 0% of each run, Pallas kernels for 0% -> 0%
where the time goes in v1:
time: 127 us
  Pallas kernels  117 us (92%)
  local copies, waits for them, and re-layouts  8.88 us (7%)
    pallas_call x1, Pallas kernels, exchange(): pl.pallas_call(exchange_kernel, out_shape=(jax.ShapeDtypeStruct((ROWS, 25...  98.4 us
    pallas_call x1, Pallas kernels, attend(): pl.pallas_call(attend_kernel, out_shape=jax.ShapeDtypeStruct((ROWS, q_raw...  18.9 us
    unnamed x17, local copies, waits for them, and re-layouts  7.31 us

profile of v1, /device:TPU:2, one launch (start us, length us, event | category | flops | bytes accessed | tf_op | source)
XLA Modules:
  0.0 127.1 jit_solution(12555765506676516827)
XLA Ops:
  0.7 1.4 %copy.12.ids_sm = s32[16,8]{1,0:T(8,128)} copy(s32[16,8]{0,1:T(8,128)} %param.11) | data formatting | bytes 1024 | tf_op args[4]
  2.0 0.1 multiply_cosine_fusion
  2.1 0.1 pad_maximum_fusion
  2.2 1.6 %copy.11.pos_ref = s32[576,1]{1,0:T(8,128)} copy(s32[576,1]{0,1:T(1,128)} %bitcast.4) | data formatting | bytes 4608 | tf_op jit(solution)/shard_map/reshape | solution.py:483
  3.8 0.0 copy-start
  3.8 0.0 copy-start.1
  3.8 0.0 copy-start.2
  3.8 98.4 %exchange.1 = (f32[576,256]{1,0:T(8,128)}, bf16[576,256]{1,0:T(8,128)(2,1)}, f32[640,8]{1,0:T(8,128)}, f32[576,256]{1,0:T(8,128)}, bf16[16,384,256]{2,1,0:T(8,128)(2,1)}) custom-call(s32[16,8]{1,0:T(8,128)} %copy.12.ids_sm, s32[576,1]{1,0:T(8,128)} %copy.11.pos_ref, bf16[576,512]{1,0:T(8,128)(2,1)} %bitcast.6, bf16[2,8,512,256]{3,2,1,0:T(8,128)(2,1)} %bitcast.5, ...), custom_call_target="tpu_custom_call" | custom-call | flops 3000000000 | bytes 10000000 | tf_op jit(solution)/shard_map/exchange/pallas_call | solution.py:447
  102.2 0.0 copy-done
  102.3 0.0 copy-done.1
  102.3 0.0 copy-done.2
  102.3 0.0 copy-start.3
  102.3 1.9 %copy-done.3 = bf16[16,384,256]{2,1,0:T(8,128)(2,1)S(1)} copy-done((bf16[16,384,256]{2,1,0:T(8,128)(2,1)S(1)}, bf16[16,384,256]{2,1,0:T(8,128)(2,1)}, u32[]{:S(2)}) %copy-start.3) | copy-done | bytes 3145752
  104.2 0.0 copy-start.4
  104.2 1.1 copy-done.4
  105.2 0.0 copy-start.5
  105.2 1.1 copy-done.5
  106.3 0.0 copy-start.6
  106.3 1.0 copy-done.6
  107.3 0.0 copy-start.7
  107.3 1.0 copy-done.7
  108.2 18.9 %attend.1 = bf16[576,256]{1,0:T(8,128)(2,1)} custom-call(s32[16,8]{1,0:T(8,128)S(1)} %copy-done.1, s32[1,576]{1,0:T(1,128)S(1)} %copy-done.2, s32[1]{0:T(128)S(6)} %copy.14.count_sm, f32[576,256]{1,0:T(8,128)S(1)} %copy-done.4, bf16[576,256]{1,0:T(8,128)(2,1)S(1)} %copy-done.7, f32[640,8]{1,0:T(8,128)S(1)} %copy-done.6, s32[576,1]{1,0:T(8,128)S(1)} %copy-done, ...), custom_call_target="tpu_custom_call" | custom-call | flops 2000000000 | bytes 5000000 | tf_op jit(solution)/shard_map/attend/pallas_call | solution.py:123
  (3 shorter events, 0.0 us)
Async XLA Ops:
  3.8 98.5 %copy-start = (s32[576,1]{1,0:T(8,128)S(1)}, s32[576,1]{1,0:T(8,128)}, u32[]{:S(2)}) copy-start(s32[576,1]{1,0:T(8,128)} %copy.11.pos_ref) | copy-start | bytes 6916
  3.8 98.5 %copy-start.1 = (s32[16,8]{1,0:T(8,128)S(1)}, s32[16,8]{1,0:T(8,128)}, u32[]{:S(2)}) copy-start(s32[16,8]{1,0:T(8,128)} %copy.12.ids_sm) | copy-start | bytes 1540
  3.8 98.5 %copy-start.2 = (s32[1,576]{1,0:T(1,128)S(1)}, s32[1,576]{1,0:T(1,128)}, u32[]{:S(2)}) copy-start(s32[1,576]{1,0:T(1,128)} %pos_sm.1) | copy-start | bytes 6916
  102.3 1.9 %copy-start.3 = (bf16[16,384,256]{2,1,0:T(8,128)(2,1)S(1)}, bf16[16,384,256]{2,1,0:T(8,128)(2,1)}, u32[]{:S(2)}) copy-start(bf16[16,384,256]{2,1,0:T(8,128)(2,1)} %get-tuple-element.14.incoming_ref) | copy-start | bytes 9437188
  104.2 1.1 copy-start.4
  105.2 1.1 copy-start.5
  106.3 1.0 copy-start.6
  107.3 1.0 copy-start.7

commit v2 on v1

v2 whole, which is shorter than its diff:
```python
import math

import jax
import jax.numpy as jnp
from jax import lax
from jax.experimental import pallas as pl
from jax.experimental.pallas import tpu as pltpu
from jax.sharding import PartitionSpec as P

D = 8192
KV_HEADS = 4
HEAD_DIM = 128
PASSAGE = 384
PASSAGES = 8
SEQ = 3072
ROWS = 576
ROPE_BASE = 1000000.0
EPSILON = 1e-06
BLOCK = 192
SPAN = 2 * PASSAGE
NEG = -1e30
FAR = 1 << 20


def turned(vectors, cosine, sine):
    return vectors * cosine + pltpu.roll(vectors, HEAD_DIM // 2, 1) * sine


def turn_tables(positions):
    half = HEAD_DIM // 2
    frequency = ROPE_BASE ** (-(jnp.arange(half, dtype=jnp.float32) * 2.0) / HEAD_DIM)
    angles = positions.astype(jnp.float32)[..., None] * frequency
    cosine, sine = jnp.cos(angles), jnp.sin(angles)
    return jnp.concatenate([cosine, cosine, -sine, sine], axis=-1)


def attend_kernel(
    ids_sm, pos_sm, count_sm, q_hbm, kv_hbm, meta_hbm, table_hbm, old_table_ref, incoming_hbm,
    out_ref, q_in, kv_in, meta_ref, table_ref, old_ref, q_s, nk_s, nv_s, kk_s, vv_s, kp_s, acc_s,
    sem, old_sem,
):
    heads = q_in.shape[1] // HEAD_DIM
    store = lax.axis_index("store")
    fetched = [
        pltpu.make_async_copy(source, target, sem.at[i])
        for i, (source, target) in enumerate(
            ((meta_hbm, meta_ref), (kv_hbm, kv_in), (table_hbm, table_ref), (q_hbm, q_in))
        )
    ]
    fetched[0].start()
    olds = [
        pltpu.make_async_copy(incoming_hbm.at[ids_sm[store, k] // 4], old_ref.at[k], old_sem.at[k])
        for k in range(PASSAGES)
    ]
    for copy in olds + fetched[1:]:
        copy.start()
    count = count_sm[0]
    fetched[0].wait()
    inverse = meta_ref[:ROWS, :1]
    spot = meta_ref[:ROWS, 1:2].astype(jnp.int32)
    row_ids = lax.broadcasted_iota(jnp.int32, (ROWS, 1), 0)
    marked = jnp.where(row_ids < count, spot, -1)
    nv_s[:, HEAD_DIM:] = jnp.ones_like(nv_s[:, HEAD_DIM:])
    vv_s[:, HEAD_DIM:] = jnp.ones_like(vv_s[:, HEAD_DIM:])

    def mark(k, carry):
        here = k * PASSAGE + lax.broadcasted_iota(jnp.int32, (1, PASSAGE), 1)
        hit = jnp.max(jnp.where(marked == here, FAR, 0), axis=0, keepdims=True)
        kp_s[:, pl.ds(pl.multiple_of(k * PASSAGE, 128), PASSAGE)] = jnp.broadcast_to(
            jnp.maximum(here, hit), (8, PASSAGE)
        )
        return carry

    lax.fori_loop(0, PASSAGES, mark, 0)
    for k in range(PASSAGES):
        olds[k].wait()

    def prepare(k, carry):
        block = old_ref[k]
        table = old_table_ref[k]
        keys = block[:, :HEAD_DIM].astype(jnp.float32)
        rows = pl.ds(pl.multiple_of(k * PASSAGE, PASSAGE), PASSAGE)
        kk_s[rows] = turned(keys, table[:, :HEAD_DIM], table[:, HEAD_DIM:]).astype(jnp.bfloat16)
        vv_s[rows, :HEAD_DIM] = block[:, HEAD_DIM:]
        return carry

    lax.fori_loop(0, PASSAGES, prepare, 0)
    for copy in fetched[1:]:
        copy.wait()
    cosine, sine = table_ref[:, :HEAD_DIM], table_ref[:, HEAD_DIM:]
    scale = HEAD_DIM**-0.5 * math.log2(math.e)
    for h in range(heads):
        part = q_in[:, h * HEAD_DIM : (h + 1) * HEAD_DIM] * inverse
        q_s[h] = (turned(part, cosine, sine) * scale).astype(jnp.bfloat16)
    fresh = kv_in[:, :HEAD_DIM].astype(jnp.float32) * inverse
    nk_s[:ROWS] = turned(fresh, cosine, sine).astype(jnp.bfloat16)
    nk_s[ROWS:] = jnp.zeros_like(nk_s[ROWS:])
    nv_s[:ROWS, :HEAD_DIM] = (kv_in[:, HEAD_DIM:].astype(jnp.float32) * inverse).astype(jnp.bfloat16)
    nv_s[ROWS:, :HEAD_DIM] = jnp.zeros_like(nv_s[ROWS:, :HEAD_DIM])
    contract = (((1,), (1,)), ((), ()))
    for b in range(ROWS // BLOCK):
        low, high = b * BLOCK, (b + 1) * BLOCK
        rows = heads * BLOCK

        @pl.when(low >= count)
        def _():
            out_ref[low:high] = jnp.zeros_like(out_ref[low:high])

        @pl.when(low < count)
        def _():
            queries = q_s[:, low:high].reshape(rows, HEAD_DIM)
            width = -(-high // 128) * 128
            scores = lax.dot_general(
                queries, nk_s[:width], contract, preferred_element_type=jnp.float32
            )
            row_of = low + lax.broadcasted_iota(jnp.int32, (BLOCK, width), 0)
            key_of = lax.broadcasted_iota(jnp.int32, (BLOCK, width), 1)
            seen = jnp.concatenate([key_of <= row_of] * heads, axis=0)
            scores = jnp.where(seen, scores, NEG)
            top = jnp.max(scores, axis=1, keepdims=True)
            weight = jnp.exp2(scores - top).astype(jnp.bfloat16)
            acc_s[...] = jnp.dot(weight, nv_s[:width], preferred_element_type=jnp.float32)
            place = spot[low:high]
            place = jnp.concatenate([place] * heads, axis=0)
            last = jnp.minimum(count, high) - 1

            def old(i, top):
                span = pl.ds(pl.multiple_of(i * SPAN, SPAN), SPAN)
                scores = lax.dot_general(
                    queries, kk_s[span], contract, preferred_element_type=jnp.float32
                )
                scores = jnp.where(kp_s[0:1, span] <= place, scores, NEG)
                risen = jnp.maximum(top, jnp.max(scores, axis=1, keepdims=True))
                weight = jnp.exp2(scores - risen).astype(jnp.bfloat16)
                part = jnp.dot(weight, vv_s[span], preferred_element_type=jnp.float32)
                acc_s[...] = acc_s[...] * jnp.exp2(top - risen) + part
                return risen

            lax.fori_loop(0, pos_sm[0, last] // SPAN + 1, old, top)
            result = acc_s[:, :HEAD_DIM] / acc_s[:, HEAD_DIM:]
            live = low + lax.broadcasted_iota(jnp.int32, (BLOCK, HEAD_DIM), 0) < count
            for h in range(heads):
                piece = jnp.where(live, result[h * BLOCK : (h + 1) * BLOCK], 0.0)
                out_ref[low:high, h * HEAD_DIM : (h + 1) * HEAD_DIM] = piece.astype(jnp.bfloat16)


def attend(passage_ids, select_index, select_count, q_raw, kv_raw, meta, table, incoming):
    heads = q_raw.shape[1] // HEAD_DIM
    old_table = turn_tables(jnp.arange(PASSAGES) * PASSAGE)[:, None]
    smem = pl.BlockSpec(memory_space=pltpu.SMEM)
    vmem = pl.BlockSpec(memory_space=pltpu.VMEM)
    hbm = pl.BlockSpec(memory_space=pl.ANY)
    return pl.pallas_call(
        attend_kernel,
        out_shape=jax.ShapeDtypeStruct((ROWS, q_raw.shape[1]), jnp.bfloat16),
        in_specs=[smem] * 3 + [hbm] * 4 + [vmem, hbm],
        out_specs=vmem,
        scratch_shapes=[
            pltpu.VMEM(q_raw.shape, q_raw.dtype),
            pltpu.VMEM(kv_raw.shape, kv_raw.dtype),
            pltpu.VMEM(meta.shape, meta.dtype),
            pltpu.VMEM(table.shape, table.dtype),
            pltpu.VMEM((PASSAGES, PASSAGE, 2 * HEAD_DIM), jnp.bfloat16),
            pltpu.VMEM((heads, ROWS, HEAD_DIM), jnp.bfloat16),
            pltpu.VMEM((640, HEAD_DIM), jnp.bfloat16),
            pltpu.VMEM((640, 2 * HEAD_DIM), jnp.bfloat16),
            pltpu.VMEM((SEQ, HEAD_DIM), jnp.bfloat16),
            pltpu.VMEM((SEQ, 2 * HEAD_DIM), jnp.bfloat16),
            pltpu.VMEM((8, SEQ), jnp.int32),
            pltpu.VMEM((heads * BLOCK, 2 * HEAD_DIM), jnp.float32),
            pltpu.SemaphoreType.DMA((4,)),
            pltpu.SemaphoreType.DMA((PASSAGES,)),
        ],
        name="attend",
        cost_estimate=pl.CostEstimate(flops=2 * 10**9, bytes_accessed=5 * 10**6, transcendentals=0),
        compiler_params=pltpu.CompilerParams(vmem_limit_bytes=56 << 20),
    )(passage_ids, select_index, select_count, q_raw, kv_raw, meta, table, old_table, incoming)


RELS = (1, 7, 2, 6, 3, 5, 4)
SLOTS = (0, 1, 3, 4, 5, 6, 7)
KV_SLOT, OWN_SLOT = 2, 8
GROUPS = ((0, 3), (3, 2), (5, 2), (7, 1))
UP_SLOTS = (1, 4, 6, 7, 5, 3, 0, OWN_SLOT)
DOWN_SLOTS = (0, 3, 5, 7, 6, 4, 1, OWN_SLOT)
KV_PARTS = ((0, 48), (48, 32), (80, 32), (112, 32))
FLOWS = 4
ORDER = (0, 2, 1, 3)
ROUTES = ((1, 1), (3, 0), (2, 1), (1, 0), (3, 1), (2, 0), (0, 1))
SHARE = ROWS // FLOWS
STEPS = 7
MESH = pl.DeviceIdType.MESH


def exchange_kernel(
    ids_sm, pos_ref, hidden_ref, query_ref, keyvalue_ref, cache_ref,
    q_ref, kv_ref, meta_ref, table_ref, incoming_ref,
    held, weights, kv_own, pool, outgoing, sending, arriving, partial, squares, fresh, places,
    local_sem, h_send, h_recv, z_send, z_recv, k_send, k_recv,
    x_send, x_recv, f_send, f_recv, d_send, d_recv, r_send, r_recv,
    s_send, s_recv, g_send, g_recv, p_send, p_recv,
):
    store = lax.axis_index("store")
    rank = lax.axis_index("tp")
    x, high, core = store // 4, (store // 2) % 2, store % 2
    low, z = rank // 8, rank % 8
    quarter = z % 4
    head = rank // 4

    def place(to_x=x, to_core=core, to_low=low, to_z=z, to_high=high):
        return (to_x * 4 + to_high * 2 + to_core, to_low * 8 + to_z)

    def remote(source, target, send, recv, device):
        return pltpu.make_async_remote_copy(
            src_ref=source, dst_ref=target, send_sem=send, recv_sem=recv,
            device_id=device, device_id_type=MESH,
        )

    def piece(owner):
        return pl.ds(pl.multiple_of(owner * 64, 64), 64)

    locals_ = [
        pltpu.make_async_copy(hidden_ref, held.at[low], local_sem.at[0]),
        pltpu.make_async_copy(cache_ref.at[:, head], pool, local_sem.at[1]),
        pltpu.make_async_copy(query_ref.at[:, z], weights.at[OWN_SLOT], local_sem.at[2]),
    ]
    for h in range(2):
        columns = pl.ds(pl.multiple_of((low * 2 + h) * 256, 256), 256)
        locals_.append(
            pltpu.make_async_copy(
                keyvalue_ref.at[:, columns], kv_own.at[h], local_sem.at[3 + h]
            )
        )
    for copy in locals_:
        copy.start()

    barrier = pltpu.get_barrier_semaphore()
    for d in range(1, 16):
        pl.semaphore_signal(
            barrier, inc=1, device_id=((store + d) % 16, rank), device_id_type=MESH
        )
    for d in range(1, 8):
        pl.semaphore_signal(
            barrier, inc=1, device_id=place(to_z=(z + d) % 8), device_id_type=MESH
        )
    pl.semaphore_signal(barrier, inc=1, device_id=place(to_low=1 - low), device_id_type=MESH)
    pl.semaphore_wait(barrier, 23)

    across = place(to_low=1 - low)
    rows_of = remote(hidden_ref, held.at[low], h_send, h_recv, across)
    mine = piece(x * 2 + core)
    spread = [remote(
        query_ref.at[:, (z + 8 - rel) % 8, mine], weights.at[SLOTS[o], :, mine],
        z_send.at[o], z_recv.at[o], place(to_z=(z + 8 - rel) % 8),
    ) for o, rel in enumerate(RELS)]
    kv_rows = []
    for h in range(2):
        columns = pl.ds(pl.multiple_of(((1 - low) * 2 + h) * 256, 256), 256)
        kv_rows.append(remote(
            keyvalue_ref.at[mine, columns], weights.at[KV_SLOT, h, mine],
            k_send.at[h], k_recv.at[h], across,
        ))
    for copy in kv_rows + spread[:2] + [rows_of] + spread[2:]:
        copy.start()

    turn = 1 - 2 * core
    owners = (x, (x + 3) % 4, (x + 1) % 4, (x + 2) % 4)

    def group(g, owner):
        start, size = GROUPS[g]
        return weights.at[pl.ds(start, size), :, piece(owner * 2 + core)]

    def beside(g, way):
        to = (x + 1) % 4 if way == 0 else (x + 3) % 4
        return remote(
            group(g, x), group(g, x), x_send.at[g, way], x_recv.at[g, way], place(to_x=to)
        )

    def onward(g):
        owner = (x + 4 - turn) % 4
        to = (x + 4 + turn) % 4
        return remote(group(g, owner), group(g, owner), f_send.at[g], f_recv.at[g], place(to_x=to))

    def twin(g, i):
        block = group(g, owners[i])
        return remote(block, block, d_send.at[g, i], d_recv.at[g, i], place(to_core=1 - core))

    def first(g):
        for copy in (spread[:2] + kv_rows, spread[2:4], spread[4:6], spread[6:])[g]:
            copy.wait_recv()
        beside(g, 0).start()
        beside(g, 1).start()
        twin(g, 0).start()

    def second(g):
        beside(g, 0).wait_recv()
        beside(g, 1).wait_recv()
        onward(g).start()
        twin(g, 1).start()
        twin(g, 2).start()

    def third(g):
        onward(g).wait_recv()
        twin(g, 3).start()

    def fourth(g):
        for i in range(4):
            twin(g, i).wait_recv()

    locals_[1].wait()

    def choose(d, carry):
        to = (store + d) % 16
        slot = jnp.int32(0)
        for k in range(PASSAGES):
            entry = ids_sm[to, k]
            slot = slot + jnp.where(entry // 4 == store, entry % 4, 0)
        outgoing[d] = pool[slot]
        return carry

    lax.fori_loop(0, 16, choose, 0)
    places[...] = jnp.zeros_like(places)
    places[:, :ROWS] = jnp.broadcast_to(pos_ref[...].astype(jnp.float32), (8, ROWS))
    half_dim = HEAD_DIM // 2
    lane = lax.broadcasted_iota(jnp.int32, (1, HEAD_DIM), 1)
    frequency = jnp.exp(
        (lane % half_dim).astype(jnp.float32) * (-2.0 * math.log(ROPE_BASE) / HEAD_DIM)
    )
    angles = jnp.transpose(places[...])[:ROWS, :1] * frequency
    table_ref[:, :HEAD_DIM] = jnp.cos(angles)
    table_ref[:, HEAD_DIM:] = jnp.sin(angles) * jnp.where(lane < half_dim, -1.0, 1.0)
    keep = pltpu.make_async_copy(outgoing.at[0], incoming_ref.at[store], local_sem.at[5])
    keep.start()
    passages = []
    for other in range(2):
        for to_x, to_high in ROUTES + ((0, 0),) * other:
            to_x, to_high = (x + to_x) % 4, (high + to_high) % 2
            to = place(to_x=to_x, to_high=to_high, to_core=(core + other) % 2)
            i = len(passages)
            passages.append(remote(
                outgoing.at[(to[0] + 16 - store) % 16], incoming_ref.at[store],
                p_send.at[i], p_recv.at[i], to,
            ))

    first(0)
    first(1)
    second(0)
    first(2)
    second(1)
    first(3)
    third(0)
    second(2)
    fourth(0)
    locals_[0].wait()
    locals_[2].wait()
    locals_[3].wait()
    locals_[4].wait()
    rows_of.wait_recv()
    def slot_of(up, s):
        slots = UP_SLOTS if up else DOWN_SLOTS
        slot = slots[0]
        for i in range(1, STEPS + 1):
            slot = jnp.where(s == i, slots[i], slot)
        return slot

    def add_up(s):
        for way, rows, offset, size in ((0, 0, 0, 80), (1, 2 * SHARE, 80, 64)):
            slot = slot_of(way == 0, s)
            to = (z + 15 - s) % 8 if way == 0 else (z + 1 + s) % 8
            rows = pl.ds(rows, 2 * SHARE)
            kv_rows = pl.ds(pl.multiple_of((to % 4) * SHARE + offset, 16), size)
            total = jnp.zeros((2 * SHARE, 256), jnp.float32)
            for b in range(2):
                total += jnp.dot(held[b, rows], weights[slot, b], preferred_element_type=jnp.float32)
            partial[way, : 2 * SHARE] = total
            partial[way, 2 * SHARE : 2 * SHARE + size] = jnp.dot(
                held[low, kv_rows], kv_own[to // 4], preferred_element_type=jnp.float32
            ) + jnp.dot(
                held[1 - low, kv_rows],
                weights[KV_SLOT, to // 4],
                preferred_element_type=jnp.float32,
            )

    def parts_of(f):
        first_row = 2 * SHARE + (KV_PARTS[f][0] if f < 2 else KV_PARTS[f][0] - 80)
        return (
            partial[f // 2, f % 2 * SHARE : (f % 2 + 1) * SHARE],
            partial[f // 2, first_row : first_row + KV_PARTS[f][1]],
        )

    def hop(f, s):
        to = (z + 1) % 8 if f < 2 else (z + 7) % 8
        size = SHARE + KV_PARTS[f][1]
        return remote(
            sending.at[f, s, pl.ds(0, size)], arriving.at[f, s, pl.ds(0, size)],
            r_send.at[f, s], r_recv.at[f, s], place(to_z=to),
        )

    def forward(f, s, total, kv_total):
        sending[f, s, :SHARE] = total.astype(jnp.bfloat16)
        sending[f, s, SHARE : SHARE + KV_PARTS[f][1]] = kv_total.astype(jnp.bfloat16)
        hop(f, s).start()

    add_up(0)
    for f in ORDER:
        forward(f, 0, *parts_of(f))
    third(1)
    second(3)
    for copy in passages:
        copy.start()
    fourth(1)
    add_up(1)

    def relay(s):
        for f in ORDER:
            total, kv_total = parts_of(f)
            hop(f, s - 1).wait_recv()
            got = arriving[f, s - 1].astype(jnp.float32)
            size = SHARE + KV_PARTS[f][1]
            forward(f, s, total + got[:SHARE], kv_total + got[SHARE:size])

    relay(1)
    third(2)
    third(3)
    fourth(2)
    add_up(2)
    ones = jnp.ones((8, 512), jnp.bfloat16)
    along = (((1,), (1,)), ((), ()))
    sum_of = jnp.zeros((8, ROWS), jnp.float32)
    for b in range(2):
        wide = held[b].astype(jnp.float32)
        square = wide * wide
        upper = square.astype(jnp.bfloat16)
        lower = (square - upper.astype(jnp.float32)).astype(jnp.bfloat16)
        sum_of += lax.dot_general(ones, upper, along, preferred_element_type=jnp.float32)
        sum_of += lax.dot_general(ones, lower, along, preferred_element_type=jnp.float32)
    squares[z, :, :ROWS] = sum_of
    squares[z, :, ROWS:] = jnp.zeros((8, 640 - ROWS), jnp.float32)
    sums = [remote(
        squares.at[z], squares.at[z], s_send.at[d - 1], s_recv.at[d - 1],
        place(to_z=(z + d) % 8),
    ) for d in range(1, 8)]
    for copy in sums:
        copy.start()

    relay(2)
    fourth(3)
    add_up(3)

    def step(s, carry):
        relay(s)
        add_up(s + 1)
        return carry

    lax.fori_loop(3, STEPS, step, 0)
    for f in ORDER:
        offset, size = KV_PARTS[f]
        total, kv_total = parts_of(f)
        hop(f, STEPS - 1).wait_recv()
        got = arriving[f, STEPS - 1].astype(jnp.float32)
        q_ref[f * SHARE : (f + 1) * SHARE] = total + got[:SHARE]
        kv_total = kv_total + got[SHARE : SHARE + size]
        fresh[quarter, offset : offset + size] = kv_total.astype(jnp.bfloat16)
    shared = [remote(
        fresh.at[quarter], fresh.at[quarter], g_send.at[d - 1], g_recv.at[d - 1],
        place(to_z=(z // 4) * 4 + (quarter + d) % 4),
    ) for d in range(1, 4)]
    for copy in shared:
        copy.start()
    for copy in sums:
        copy.wait_recv()
    total = squares[0]
    for b in range(1, 8):
        total += squares[b]
    inverse = lax.rsqrt(total * (1.0 / D) + EPSILON)
    first_row = lax.broadcasted_iota(jnp.int32, (8, 640), 0) == 0
    meta_ref[...] = jnp.transpose(jnp.where(first_row, inverse, places[...]))
    for copy in shared:
        copy.wait_recv()
    for i in range(4):
        kv_ref[i * SHARE : (i + 1) * SHARE] = fresh[i]
    for copy in passages:
        copy.wait_recv()
    keep.wait()
    for copy in [rows_of] + spread + kv_rows + passages + sums + shared:
        copy.wait_send()
    for g in range(4):
        beside(g, 0).wait_send()
        beside(g, 1).wait_send()
        onward(g).wait_send()
        for i in range(4):
            twin(g, i).wait_send()

    def drained(s, carry):
        for f in range(FLOWS):
            hop(f, s).wait_send()
        return carry

    lax.fori_loop(0, STEPS, drained, 0)


def exchange(passage_ids, select_index, hidden, w_query, w_keyvalue, passage_cache):
    smem = pl.BlockSpec(memory_space=pltpu.SMEM)
    vmem = pl.BlockSpec(memory_space=pltpu.VMEM)
    hbm = pl.BlockSpec(memory_space=pltpu.HBM)
    dma = pltpu.SemaphoreType.DMA
    return pl.pallas_call(
        exchange_kernel,
        out_shape=(
            jax.ShapeDtypeStruct((ROWS, 256), jnp.float32),
            jax.ShapeDtypeStruct((ROWS, 256), jnp.bfloat16),
            jax.ShapeDtypeStruct((640, 8), jnp.float32),
            jax.ShapeDtypeStruct((ROWS, 2 * HEAD_DIM), jnp.float32),
            jax.ShapeDtypeStruct((16, PASSAGE, 256), jnp.bfloat16),
        ),
        in_specs=[smem, vmem, hbm, hbm, hbm, hbm],
        out_specs=(vmem, vmem, vmem, vmem, pl.BlockSpec(memory_space=pl.ANY)),
        scratch_shapes=[
            pltpu.VMEM((2, ROWS, 512), jnp.bfloat16),
            pltpu.VMEM((9, 2, 512, 256), jnp.bfloat16),
            pltpu.VMEM((2, 512, 256), jnp.bfloat16),
            pltpu.VMEM((4, PASSAGE, 256), jnp.bfloat16),
            pltpu.VMEM((16, PASSAGE, 256), jnp.bfloat16),
            pltpu.VMEM((FLOWS, STEPS, 192, 256), jnp.bfloat16),
            pltpu.VMEM((FLOWS, STEPS, 192, 256), jnp.bfloat16),
            pltpu.VMEM((2, 2 * SHARE + 80, 256), jnp.float32),
            pltpu.VMEM((8, 8, 640), jnp.float32),
            pltpu.VMEM((4, SHARE, 256), jnp.bfloat16),
            pltpu.VMEM((8, 640), jnp.float32),
            dma((6,)), dma(()), dma(()), dma((7,)), dma((7,)), dma((2,)), dma((2,)),
            dma((4, 2)), dma((4, 2)), dma((4,)), dma((4,)),
            dma((4, 4)), dma((4, 4)), dma((4, 7)), dma((4, 7)), dma((7,)), dma((7,)),
            dma((3,)), dma((3,)), dma((15,)), dma((15,)),
        ],
        name="exchange",
        cost_estimate=pl.CostEstimate(
            flops=3 * 10**9, bytes_accessed=10**7, transcendentals=0
        ),
        compiler_params=pltpu.CompilerParams(
            collective_id=0, has_side_effects=True, vmem_limit_bytes=56 << 20
        ),
    )(
        passage_ids,
        select_index,
        hidden.reshape(ROWS, 512),
        w_query.reshape(2, 8, 512, 256),
        w_keyvalue,
        passage_cache,
    )


def local(hidden, w_query, w_keyvalue, passage_cache, passage_ids, select_index, select_count):
    q_raw, kv_raw, meta, table, incoming = exchange(
        passage_ids, select_index, hidden, w_query, w_keyvalue, passage_cache
    )
    context = attend(
        passage_ids, select_index, select_count, q_raw, kv_raw, meta, table, incoming
    )
    return context[None]


def solution(mesh):
    placed = (
        P("store", None, "tp"),
        P(None, "tp"),
        P("tp", None),
        P("store", None, None, None),
        P(),
        P("store", None),
        P("store"),
    )
    return jax.shard_map(
        local, mesh=mesh, in_specs=placed, out_specs=P("store", None, "tp"), check_vma=False
    )
```

time: 127 us -> 96.4 us (0.76); the launches traced: 127 us -> 94.9 us
  Pallas kernels: 117 us -> 92 us
  local copies, waits for them, and re-layouts: 8.88 us -> 1.96 us
    pallas_call x1, Pallas kernels: 98.4 us -> 76.1 us  [exchange(): pl.pallas_call(exchange_kernel, out_shape=(jax.ShapeDtypeStruct((ROWS, 25...]
    unnamed x17 -> x1, local copies, waits for them, and re-layouts: 7.31 us -> 1.35 us
    pallas_call x1, Pallas kernels: 18.9 us -> 15.9 us  [attend(): pl.pallas_call(attend_kernel, out_shape=jax.ShapeDtypeStruct((ROWS, q_raw...]
    reshape x1 -> x0, local copies, waits for them, and re-layouts: 1.56 us -> none  [exchange(): select_index.reshape(ROWS, 1)]
where the time goes in v2:
time: 96.4 us; the launch traced here: 94.9 us
  Pallas kernels  92 us (95%)
  local copies, waits for them, and re-layouts  1.96 us (2%)
    pallas_call x1, Pallas kernels, exchange(): pl.pallas_call(exchange_kernel, out_shape=(jax.ShapeDtypeStruct((ROWS, 25...  76.1 us
    pallas_call x1, Pallas kernels, attend(): pl.pallas_call(attend_kernel, out_shape=jax.ShapeDtypeStruct((ROWS, q_raw...  15.9 us

profile of v2, /device:TPU:2, one launch (start us, length us, event | category | flops | bytes accessed | tf_op | source)
XLA Modules:
  0.0 94.9 jit_solution(12646273164201036999)
XLA Ops:
  0.7 1.4 %copy.9.ids_sm = s32[16,8]{1,0:T(8,128)} copy(s32[16,8]{0,1:T(8,128)} %param.11) | data formatting | bytes 1024 | tf_op args[4]
  2.0 0.1 multiply_cosine_fusion
  2.1 0.1 pad_maximum_fusion
  2.2 0.6 broadcast_in_dim.8.old_table_ref
  2.8 76.1 %exchange.1 = (f32[576,256]{1,0:T(8,128)}, bf16[576,256]{1,0:T(8,128)(2,1)}, f32[640,8]{1,0:T(8,128)}, f32[576,256]{1,0:T(8,128)}, bf16[16,384,256]{2,1,0:T(8,128)(2,1)}) custom-call(s32[16,8]{1,0:T(8,128)} %copy.9.ids_sm, s32[1,576]{1,0:T(1,128)} %pos_sm.1, bf16[576,512]{1,0:T(8,128)(2,1)} %bitcast.4, bf16[2,8,512,256]{3,2,1,0:T(8,128)(2,1)} %bitcast.3, ...), custom_call_target="tpu_custom_call" | custom-call | flops 3000000000 | bytes 10000000 | tf_op jit(solution)/shard_map/exchange/pallas_call | solution.py:507
  78.9 15.9 %attend.1 = bf16[576,256]{1,0:T(8,128)(2,1)} custom-call(s32[16,8]{1,0:T(8,128)} %copy.9.ids_sm, s32[1,576]{1,0:T(1,128)} %pos_sm.1, s32[1]{0:T(128)S(6)} %copy.10.count_sm, f32[576,256]{1,0:T(8,128)} %get-tuple-element.10.q_hbm, bf16[576,256]{1,0:T(8,128)(2,1)} %get-tuple-element.11.kv_hbm, f32[640,8]{1,0:T(8,128)} %get-tuple-element.12.meta_hbm, ...), custom_call_target="tpu_custom_call" | custom-call | flops 2000000000 | bytes 5000000 | tf_op jit(solution)/shard_map/attend/pallas_call | solution.py:153
  (2 shorter events, 0.0 us)

commit v3 on v2

v3 whole, which is shorter than its diff:
```python
import math

import jax
import jax.numpy as jnp
from jax import lax
from jax.experimental import pallas as pl
from jax.experimental.pallas import tpu as pltpu
from jax.sharding import PartitionSpec as P

D = 8192
KV_HEADS = 4
HEAD_DIM = 128
PASSAGE = 384
PASSAGES = 8
SEQ = 3072
ROWS = 576
ROPE_BASE = 1000000.0
EPSILON = 1e-06
BLOCK = 192
SPAN = 2 * PASSAGE
NEG = -1e30
CONTRACT = (((1,), (1,)), ((), ()))
FAR = 1 << 20


def turned(vectors, cosine, sine):
    return vectors * cosine + pltpu.roll(vectors, HEAD_DIM // 2, 1) * sine


def turn_tables(positions):
    half = HEAD_DIM // 2
    frequency = ROPE_BASE ** (-(jnp.arange(half, dtype=jnp.float32) * 2.0) / HEAD_DIM)
    angles = positions.astype(jnp.float32)[..., None] * frequency
    cosine, sine = jnp.cos(angles), jnp.sin(angles)
    return jnp.concatenate([cosine, cosine, -sine, sine], axis=-1)


def attend_kernel(
    slots_sm, pos_sm, count_sm, q_hbm, acc_hbm, marks_hbm, meta_hbm, old_table_ref, incoming_hbm,
    out_ref, q_s, acc_in, kp_s, meta_ref, old_ref, kk_s, vv_s, acc_s, sem, old_sem,
):
    heads = q_s.shape[0]
    olds = [
        pltpu.make_async_copy(incoming_hbm.at[slots_sm[0, k]], old_ref.at[k], old_sem.at[k])
        for k in range(PASSAGES)
    ]
    fetched = [
        pltpu.make_async_copy(source, target, sem.at[i])
        for i, (source, target) in enumerate(
            ((q_hbm, q_s), (acc_hbm, acc_in), (marks_hbm, kp_s), (meta_hbm, meta_ref))
        )
    ]
    for copy in olds + fetched:
        copy.start()
    count = count_sm[0]
    vv_s[:, HEAD_DIM:] = jnp.ones_like(vv_s[:, HEAD_DIM:])
    for k in range(PASSAGES):
        olds[k].wait()
        block = old_ref[k]
        table = old_table_ref[k]
        keys = block[:, :HEAD_DIM].astype(jnp.float32)
        rows = slice(k * PASSAGE, (k + 1) * PASSAGE)
        kk_s[rows] = turned(keys, table[:, :HEAD_DIM], table[:, HEAD_DIM:]).astype(jnp.bfloat16)
        vv_s[rows, :HEAD_DIM] = block[:, HEAD_DIM:]
    for copy in fetched:
        copy.wait()
    for b in range(ROWS // BLOCK):
        low, high = b * BLOCK, (b + 1) * BLOCK

        @pl.when(low >= count)
        def _():
            out_ref[low:high] = jnp.zeros_like(out_ref[low:high])

        @pl.when(low < count)
        def _():
            acc_s[...] = acc_in[b]
            tops = [acc_in[b, h * BLOCK : (h + 1) * BLOCK, 2 * HEAD_DIM - 1 :] for h in range(heads)]
            place = meta_ref[low:high, 1:2].astype(jnp.int32)
            last = jnp.minimum(count, high) - 1

            def old(i, tops):
                span = pl.ds(pl.multiple_of(i * SPAN, SPAN), SPAN)
                seen = kp_s[0:1, span] <= place
                raw = [
                    lax.dot_general(
                        q_s[h, low:high], kk_s[span], CONTRACT, preferred_element_type=jnp.float32
                    )
                    for h in range(heads)
                ]
                risen_tops = []
                for h, top in enumerate(tops):
                    mine = slice(h * BLOCK, (h + 1) * BLOCK)
                    scores = jnp.where(seen, raw[h], NEG)
                    risen = jnp.maximum(top, jnp.max(scores, axis=1, keepdims=True))
                    weight = jnp.exp2(scores - risen).astype(jnp.bfloat16)
                    part = jnp.dot(weight, vv_s[span], preferred_element_type=jnp.float32)
                    acc_s[mine] = acc_s[mine] * jnp.exp2(top - risen) + part
                    risen_tops.append(risen)
                return tuple(risen_tops)

            lax.fori_loop(0, pos_sm[0, last] // SPAN + 1, old, tuple(tops))
            result = acc_s[:, :HEAD_DIM] / acc_s[:, HEAD_DIM : HEAD_DIM + 1]
            live = low + lax.broadcasted_iota(jnp.int32, (BLOCK, HEAD_DIM), 0) < count
            for h in range(heads):
                piece = jnp.where(live, result[h * BLOCK : (h + 1) * BLOCK], 0.0)
                out_ref[low:high, h * HEAD_DIM : (h + 1) * HEAD_DIM] = piece.astype(jnp.bfloat16)


def attend(slots, select_index, select_count, queries, begun, marks, meta, incoming):
    heads = queries.shape[0]
    old_table = turn_tables(jnp.arange(PASSAGES) * PASSAGE)[:, None]
    smem = pl.BlockSpec(memory_space=pltpu.SMEM)
    vmem = pl.BlockSpec(memory_space=pltpu.VMEM)
    hbm = pl.BlockSpec(memory_space=pl.ANY)
    return pl.pallas_call(
        attend_kernel,
        out_shape=jax.ShapeDtypeStruct((ROWS, heads * HEAD_DIM), jnp.bfloat16),
        in_specs=[smem] * 3 + [hbm] * 4 + [vmem, hbm],
        out_specs=vmem,
        scratch_shapes=[
            pltpu.VMEM(queries.shape, queries.dtype),
            pltpu.VMEM(begun.shape, begun.dtype),
            pltpu.VMEM(marks.shape, marks.dtype),
            pltpu.VMEM(meta.shape, meta.dtype),
            pltpu.VMEM((PASSAGES, PASSAGE, 2 * HEAD_DIM), jnp.bfloat16),
            pltpu.VMEM((SEQ, HEAD_DIM), jnp.bfloat16),
            pltpu.VMEM((SEQ, 2 * HEAD_DIM), jnp.bfloat16),
            pltpu.VMEM((heads * BLOCK, 2 * HEAD_DIM), jnp.float32),
            pltpu.SemaphoreType.DMA((4,)),
            pltpu.SemaphoreType.DMA((PASSAGES,)),
        ],
        name="attend",
        cost_estimate=pl.CostEstimate(flops=2 * 10**9, bytes_accessed=5 * 10**6, transcendentals=0),
        compiler_params=pltpu.CompilerParams(vmem_limit_bytes=56 << 20),
    )(slots, select_index, select_count, queries, begun, marks, meta, old_table, incoming)


RELS = (1, 7, 2, 6, 3, 5, 4)
SLOTS = (0, 1, 3, 4, 5, 6, 7)
KV_SLOT, OWN_SLOT = 2, 8
GROUPS = ((0, 3), (3, 2), (5, 2), (7, 1))
UP_SLOTS = (1, 4, 6, 7, 5, 3, 0, OWN_SLOT)
DOWN_SLOTS = (0, 3, 5, 7, 6, 4, 1, OWN_SLOT)
QUERY_FLOWS = 4
FLOWS = 6
KV_PARTS = ((0, 80), (80, 64))
SIZES = (144, 144, 144, 144, 80, 64)
ORDER = (4, 5, 0, 2, 1, 3)
ROUTES = ((1, 1), (3, 0), (2, 1), (1, 0), (3, 1), (2, 0), (0, 1))
SHARE = ROWS // QUERY_FLOWS
STEPS = 7
MESH = pl.DeviceIdType.MESH


def exchange_kernel(
    ids_ref, count_sm, pos_ref, hidden_ref, query_ref, keyvalue_ref, cache_ref,
    queries_ref, begun_ref, marks_ref, meta_ref, slots_ref, incoming_ref,
    ids_sm, held, weights, kv_own, pool, outgoing, sending, arriving, partial, squares, fresh, places,
    q_raw, table_ref, nk_s, nv_s,
    local_sem, h_send, h_recv, z_send, z_recv, k_send, k_recv,
    x_send, x_recv, f_send, f_recv, d_send, d_recv, r_send, r_recv,
    s_send, s_recv, g_send, g_recv, p_send, p_recv,
):
    store = lax.axis_index("store")
    rank = lax.axis_index("tp")
    x, high, core = store // 4, (store // 2) % 2, store % 2
    low, z = rank // 8, rank % 8
    quarter = z % 4
    head = rank // 4

    def place(to_x=x, to_core=core, to_low=low, to_z=z, to_high=high):
        return (to_x * 4 + to_high * 2 + to_core, to_low * 8 + to_z)

    def remote(source, target, send, recv, device):
        return pltpu.make_async_remote_copy(
            src_ref=source, dst_ref=target, send_sem=send, recv_sem=recv,
            device_id=device, device_id_type=MESH,
        )

    def piece(owner):
        return pl.ds(pl.multiple_of(owner * 64, 64), 64)

    locals_ = [
        pltpu.make_async_copy(hidden_ref, held.at[low], local_sem.at[0]),
        pltpu.make_async_copy(cache_ref.at[:, head], pool, local_sem.at[1]),
        pltpu.make_async_copy(query_ref.at[:, z], weights.at[OWN_SLOT], local_sem.at[2]),
    ]
    for h in range(2):
        columns = pl.ds(pl.multiple_of((low * 2 + h) * 256, 256), 256)
        locals_.append(
            pltpu.make_async_copy(
                keyvalue_ref.at[:, columns], kv_own.at[h], local_sem.at[3 + h]
            )
        )
    locals_.append(pltpu.make_async_copy(ids_ref, ids_sm, local_sem.at[6]))
    for copy in locals_:
        copy.start()

    barrier = pltpu.get_barrier_semaphore()
    for d in range(1, 16):
        pl.semaphore_signal(
            barrier, inc=1, device_id=((store + d) % 16, rank), device_id_type=MESH
        )
    for d in range(1, 8):
        pl.semaphore_signal(
            barrier, inc=1, device_id=place(to_z=(z + d) % 8), device_id_type=MESH
        )
    pl.semaphore_signal(barrier, inc=1, device_id=place(to_low=1 - low), device_id_type=MESH)
    pl.semaphore_wait(barrier, 23)

    across = place(to_low=1 - low)
    rows_of = remote(hidden_ref, held.at[low], h_send, h_recv, across)
    mine = piece(x * 2 + core)
    spread = [remote(
        query_ref.at[:, (z + 8 - rel) % 8, mine], weights.at[SLOTS[o], :, mine],
        z_send.at[o], z_recv.at[o], place(to_z=(z + 8 - rel) % 8),
    ) for o, rel in enumerate(RELS)]
    kv_rows = []
    for h in range(2):
        columns = pl.ds(pl.multiple_of(((1 - low) * 2 + h) * 256, 256), 256)
        kv_rows.append(remote(
            keyvalue_ref.at[mine, columns], weights.at[KV_SLOT, h, mine],
            k_send.at[h], k_recv.at[h], across,
        ))
    for copy in kv_rows + spread[:2] + [rows_of] + spread[2:]:
        copy.start()

    turn = 1 - 2 * core
    owners = (x, (x + 3) % 4, (x + 1) % 4, (x + 2) % 4)

    def group(g, owner):
        start, size = GROUPS[g]
        return weights.at[pl.ds(start, size), :, piece(owner * 2 + core)]

    def beside(g, way):
        to = (x + 1) % 4 if way == 0 else (x + 3) % 4
        return remote(
            group(g, x), group(g, x), x_send.at[g, way], x_recv.at[g, way], place(to_x=to)
        )

    def onward(g):
        owner = (x + 4 - turn) % 4
        to = (x + 4 + turn) % 4
        return remote(group(g, owner), group(g, owner), f_send.at[g], f_recv.at[g], place(to_x=to))

    def twin(g, i):
        block = group(g, owners[i])
        return remote(block, block, d_send.at[g, i], d_recv.at[g, i], place(to_core=1 - core))

    def first(g):
        for copy in (spread[:2] + kv_rows, spread[2:4], spread[4:6], spread[6:])[g]:
            copy.wait_recv()
        beside(g, 0).start()
        beside(g, 1).start()
        twin(g, 0).start()

    def second(g):
        beside(g, 0).wait_recv()
        beside(g, 1).wait_recv()
        onward(g).start()
        twin(g, 1).start()
        twin(g, 2).start()

    def third(g):
        onward(g).wait_recv()
        twin(g, 3).start()

    def fourth(g):
        for i in range(4):
            twin(g, i).wait_recv()

    locals_[1].wait()
    locals_[5].wait()
    for k in range(PASSAGES):
        slots_ref[0, k] = ids_sm[k, store] // 4

    def choose(d, carry):
        to = (store + d) % 16
        slot = jnp.int32(0)
        for k in range(PASSAGES):
            entry = ids_sm[k, to]
            slot = slot + jnp.where(entry // 4 == store, entry % 4, 0)
        outgoing[d] = pool[slot]
        return carry

    lax.fori_loop(0, 16, choose, 0)
    places[...] = jnp.zeros_like(places)
    places[:, :ROWS] = jnp.broadcast_to(pos_ref[...].astype(jnp.float32), (8, ROWS))
    half_dim = HEAD_DIM // 2
    lane = lax.broadcasted_iota(jnp.int32, (1, HEAD_DIM), 1)
    frequency = jnp.exp(
        (lane % half_dim).astype(jnp.float32) * (-2.0 * math.log(ROPE_BASE) / HEAD_DIM)
    )
    spot = jnp.transpose(places[...])[:ROWS, :1]
    angles = spot * frequency
    row_ids = lax.broadcasted_iota(jnp.int32, (ROWS, 1), 0)
    marked = jnp.where(row_ids < count_sm[0], spot.astype(jnp.int32), -1)
    table_ref[:, :HEAD_DIM] = jnp.cos(angles)
    table_ref[:, HEAD_DIM:] = jnp.sin(angles) * jnp.where(lane < half_dim, -1.0, 1.0)
    for k in range(PASSAGES):
        here = k * PASSAGE + lax.broadcasted_iota(jnp.int32, (1, PASSAGE), 1)
        hit = jnp.max(jnp.where(marked == here, FAR, 0), axis=0, keepdims=True)
        marks_ref[:, k * PASSAGE : (k + 1) * PASSAGE] = jnp.broadcast_to(
            jnp.maximum(here, hit), (8, PASSAGE)
        )
    nv_s[:, HEAD_DIM:] = jnp.ones_like(nv_s[:, HEAD_DIM:])
    nk_s[ROWS:] = jnp.zeros_like(nk_s[ROWS:])
    nv_s[ROWS:, :HEAD_DIM] = jnp.zeros_like(nv_s[ROWS:, :HEAD_DIM])
    keep = pltpu.make_async_copy(outgoing.at[0], incoming_ref.at[store], local_sem.at[5])
    keep.start()
    passages = []
    for other in range(2):
        for to_x, to_high in ROUTES + ((0, 0),) * other:
            to_x, to_high = (x + to_x) % 4, (high + to_high) % 2
            to = place(to_x=to_x, to_high=to_high, to_core=(core + other) % 2)
            i = len(passages)
            passages.append(remote(
                outgoing.at[(to[0] + 16 - store) % 16], incoming_ref.at[store],
                p_send.at[i], p_recv.at[i], to,
            ))

    first(0)
    first(1)
    second(0)
    first(2)
    second(1)
    first(3)
    third(0)
    second(2)
    fourth(0)
    locals_[0].wait()
    locals_[2].wait()
    locals_[3].wait()
    locals_[4].wait()
    rows_of.wait_recv()
    def slot_of(up, s):
        slots = UP_SLOTS if up else DOWN_SLOTS
        slot = slots[0]
        for i in range(1, STEPS + 1):
            slot = jnp.where(s == i, slots[i], slot)
        return slot

    def add_up(s):
        for way, (offset, size) in enumerate(KV_PARTS):
            slot = slot_of(way == 0, s)
            to = (z + 15 - s) % 8 if way == 0 else (z + 1 + s) % 8
            rows = pl.ds(way * 2 * SHARE, 2 * SHARE)
            kv_rows = pl.ds(pl.multiple_of((to % 4) * SHARE + offset, 16), size)
            total = jnp.zeros((2 * SHARE, 256), jnp.float32)
            for b in range(2):
                total += jnp.dot(held[b, rows], weights[slot, b], preferred_element_type=jnp.float32)
            partial[way, : 2 * SHARE] = total
            partial[way, 2 * SHARE : 2 * SHARE + size] = jnp.dot(
                held[low, kv_rows], kv_own[to // 4], preferred_element_type=jnp.float32
            ) + jnp.dot(
                held[1 - low, kv_rows],
                weights[KV_SLOT, to // 4],
                preferred_element_type=jnp.float32,
            )

    def is_up(f):
        return f in (0, 1, 4)

    def part_of(f):
        if f < QUERY_FLOWS:
            return partial[f // 2, f % 2 * SHARE : (f % 2 + 1) * SHARE]
        return partial[f - QUERY_FLOWS, 2 * SHARE : 2 * SHARE + SIZES[f]]

    def hop(f, s):
        to = (z + 1) % 8 if is_up(f) else (z + 7) % 8
        rows = pl.ds(0, SIZES[f])
        return remote(
            sending.at[f, s, rows], arriving.at[f, s, rows],
            r_send.at[f, s], r_recv.at[f, s], place(to_z=to),
        )

    def forward(f, s, total):
        sending[f, s, : SIZES[f]] = total.astype(jnp.bfloat16)
        hop(f, s).start()

    add_up(0)
    for f in ORDER:
        forward(f, 0, part_of(f))
    third(1)
    second(3)
    for copy in passages:
        copy.start()
    fourth(1)
    add_up(1)

    def summed(f, s):
        hop(f, s).wait_recv()
        return part_of(f) + arriving[f, s, : SIZES[f]].astype(jnp.float32)

    def relay(s):
        for f in ORDER:
            forward(f, s, summed(f, s - 1))

    relay(1)
    third(2)
    third(3)
    fourth(2)
    add_up(2)
    ones = jnp.ones((8, 512), jnp.bfloat16)
    along = (((1,), (1,)), ((), ()))
    sum_of = jnp.zeros((8, ROWS), jnp.float32)
    for b in range(2):
        wide = held[b].astype(jnp.float32)
        square = wide * wide
        upper = square.astype(jnp.bfloat16)
        lower = (square - upper.astype(jnp.float32)).astype(jnp.bfloat16)
        sum_of += lax.dot_general(ones, upper, along, preferred_element_type=jnp.float32)
        sum_of += lax.dot_general(ones, lower, along, preferred_element_type=jnp.float32)
    squares[z, :, :ROWS] = sum_of
    squares[z, :, ROWS:] = jnp.zeros((8, 640 - ROWS), jnp.float32)
    sums = [remote(
        squares.at[z], squares.at[z], s_send.at[d - 1], s_recv.at[d - 1],
        place(to_z=(z + d) % 8),
    ) for d in range(1, 8)]
    for copy in sums:
        copy.start()

    relay(2)
    fourth(3)
    add_up(3)

    def step(s, carry):
        relay(s)
        add_up(s + 1)
        return carry

    lax.fori_loop(3, STEPS, step, 0)
    for f in range(QUERY_FLOWS, FLOWS):
        offset, size = KV_PARTS[f - QUERY_FLOWS]
        fresh[quarter, offset : offset + size] = summed(f, STEPS - 1).astype(jnp.bfloat16)
    shared = [remote(
        fresh.at[quarter], fresh.at[quarter], g_send.at[d - 1], g_recv.at[d - 1],
        place(to_z=(z // 4) * 4 + (quarter + d) % 4),
    ) for d in range(1, 4)]
    for copy in shared:
        copy.start()
    for f in ORDER[2:]:
        q_raw[f * SHARE : (f + 1) * SHARE] = summed(f, STEPS - 1)
    for copy in sums:
        copy.wait_recv()
    total = squares[0]
    for b in range(1, 8):
        total += squares[b]
    inverse = lax.rsqrt(total * (1.0 / D) + EPSILON)
    first_row = lax.broadcasted_iota(jnp.int32, (8, 640), 0) == 0
    meta = jnp.transpose(jnp.where(first_row, inverse, places[...]))
    meta_ref[...] = meta
    inverse = meta[:ROWS, :1]
    heads = q_raw.shape[1] // HEAD_DIM
    scale = HEAD_DIM**-0.5 * math.log2(math.e)
    for h in range(heads):
        part = q_raw[:, h * HEAD_DIM : (h + 1) * HEAD_DIM] * inverse
        part = turned(part, table_ref[:, :HEAD_DIM], table_ref[:, HEAD_DIM:])
        queries_ref[h] = (part * scale).astype(jnp.bfloat16)
    for copy in shared:
        copy.wait_recv()
    for i in range(4):
        rows = slice(i * SHARE, (i + 1) * SHARE)
        key_value = fresh[i].astype(jnp.float32) * inverse[rows]
        key = turned(key_value[:, :HEAD_DIM], table_ref[rows, :HEAD_DIM], table_ref[rows, HEAD_DIM:])
        nk_s[rows] = key.astype(jnp.bfloat16)
        nv_s[rows, :HEAD_DIM] = key_value[:, HEAD_DIM:].astype(jnp.bfloat16)
    for b in range(ROWS // BLOCK):
        begin, end = b * BLOCK, (b + 1) * BLOCK
        width = -(-end // 128) * 128
        queries = queries_ref[:, begin:end].reshape(heads * BLOCK, HEAD_DIM)
        scores = lax.dot_general(
            queries, nk_s[:width], CONTRACT, preferred_element_type=jnp.float32
        )
        row_of = begin + lax.broadcasted_iota(jnp.int32, (BLOCK, width), 0)
        key_of = lax.broadcasted_iota(jnp.int32, (BLOCK, width), 1)
        seen = jnp.concatenate([key_of <= row_of] * heads, axis=0)
        scores = jnp.where(seen, scores, NEG)
        top = jnp.max(scores, axis=1, keepdims=True)
        weight = jnp.exp2(scores - top).astype(jnp.bfloat16)
        acc = jnp.dot(weight, nv_s[:width], preferred_element_type=jnp.float32)
        last_lane = lax.broadcasted_iota(jnp.int32, acc.shape, 1) == 2 * HEAD_DIM - 1
        begun_ref[b] = jnp.where(last_lane, top, acc)
    for copy in passages:
        copy.wait_recv()
    keep.wait()
    for copy in [rows_of] + spread + kv_rows + passages + sums + shared:
        copy.wait_send()
    for g in range(4):
        beside(g, 0).wait_send()
        beside(g, 1).wait_send()
        onward(g).wait_send()
        for i in range(4):
            twin(g, i).wait_send()

    def drained(s, carry):
        for f in range(FLOWS):
            hop(f, s).wait_send()
        return carry

    lax.fori_loop(0, STEPS, drained, 0)


def exchange(passage_ids, select_count, select_index, hidden, w_query, w_keyvalue, passage_cache):
    smem = pl.BlockSpec(memory_space=pltpu.SMEM)
    vmem = pl.BlockSpec(memory_space=pltpu.VMEM)
    hbm = pl.BlockSpec(memory_space=pltpu.HBM)
    dma = pltpu.SemaphoreType.DMA
    return pl.pallas_call(
        exchange_kernel,
        out_shape=(
            jax.ShapeDtypeStruct((2, ROWS, HEAD_DIM), jnp.bfloat16),
            jax.ShapeDtypeStruct((ROWS // BLOCK, 2 * BLOCK, 256), jnp.float32),
            jax.ShapeDtypeStruct((8, SEQ), jnp.int32),
            jax.ShapeDtypeStruct((640, 8), jnp.float32),
            jax.ShapeDtypeStruct((1, PASSAGES), jnp.int32),
            jax.ShapeDtypeStruct((16, PASSAGE, 256), jnp.bfloat16),
        ),
        in_specs=[hbm, smem, vmem, hbm, hbm, hbm, hbm],
        out_specs=(vmem, vmem, vmem, vmem, smem, pl.BlockSpec(memory_space=pl.ANY)),
        scratch_shapes=[
            pltpu.SMEM((PASSAGES, 16), jnp.int32),
            pltpu.VMEM((2, ROWS, 512), jnp.bfloat16),
            pltpu.VMEM((9, 2, 512, 256), jnp.bfloat16),
            pltpu.VMEM((2, 512, 256), jnp.bfloat16),
            pltpu.VMEM((4, PASSAGE, 256), jnp.bfloat16),
            pltpu.VMEM((16, PASSAGE, 256), jnp.bfloat16),
            pltpu.VMEM((FLOWS, STEPS, SHARE, 256), jnp.bfloat16),
            pltpu.VMEM((FLOWS, STEPS, SHARE, 256), jnp.bfloat16),
            pltpu.VMEM((2, 2 * SHARE + 80, 256), jnp.float32),
            pltpu.VMEM((8, 8, 640), jnp.float32),
            pltpu.VMEM((4, SHARE, 256), jnp.bfloat16),
            pltpu.VMEM((8, 640), jnp.float32),
            pltpu.VMEM((ROWS, 256), jnp.float32),
            pltpu.VMEM((ROWS, 2 * HEAD_DIM), jnp.float32),
            pltpu.VMEM((640, HEAD_DIM), jnp.bfloat16),
            pltpu.VMEM((640, 2 * HEAD_DIM), jnp.bfloat16),
            dma((7,)), dma(()), dma(()), dma((7,)), dma((7,)), dma((2,)), dma((2,)),
            dma((4, 2)), dma((4, 2)), dma((4,)), dma((4,)),
            dma((4, 4)), dma((4, 4)), dma((6, 7)), dma((6, 7)), dma((7,)), dma((7,)),
            dma((3,)), dma((3,)), dma((15,)), dma((15,)),
        ],
        name="exchange",
        cost_estimate=pl.CostEstimate(
            flops=3 * 10**9, bytes_accessed=10**7, transcendentals=0
        ),
        compiler_params=pltpu.CompilerParams(
            collective_id=0, has_side_effects=True, vmem_limit_bytes=56 << 20
        ),
    )(
        passage_ids.T,
        select_count,
        select_index,
        hidden.reshape(ROWS, 512),
        w_query.reshape(2, 8, 512, 256),
        w_keyvalue,
        passage_cache,
    )


def local(hidden, w_query, w_keyvalue, passage_cache, passage_ids, select_index, select_count):
    queries, begun, marks, meta, slots, incoming = exchange(
        passage_ids, select_count, select_index, hidden, w_query, w_keyvalue, passage_cache
    )
    context = attend(
        slots, select_index, select_count, queries, begun, marks, meta, incoming
    )
    return context[None]


def solution(mesh):
    placed = (
        P("store", None, "tp"),
        P(None, "tp"),
        P("tp", None),
        P("store", None, None, None),
        P(),
        P("store", None),
        P("store"),
    )
    return jax.shard_map(
        local, mesh=mesh, in_specs=placed, out_specs=P("store", None, "tp"), check_vma=False
    )
```

time: 96.4 us -> 91 us (0.944)
  Pallas kernels: 92 us -> 88.2 us
  local copies, waits for them, and re-layouts: 1.96 us -> 0.61 us
    pallas_call x2, Pallas kernels: 92 us -> 88.2 us  [the longest x1 75.4 us: exchange(): pl.pallas_call(exchange_kernel, out_shape=(jax.ShapeDtypeStruct((2, ROWS,...]
    unnamed x1 -> x0, local copies, waits for them, and re-layouts: 1.35 us -> none
where the time goes in v3:
time: 91 us; the launch traced here: 89.7 us
  Pallas kernels  88.2 us (97%)
    pallas_call x1, Pallas kernels, exchange(): pl.pallas_call(exchange_kernel, out_shape=(jax.ShapeDtypeStruct((2, ROWS,...  75.4 us
    pallas_call x1, Pallas kernels, attend(): pl.pallas_call(attend_kernel, out_shape=jax.ShapeDtypeStruct((ROWS, heads...  12.8 us

profile of v3, /device:TPU:2, one launch (start us, length us, event | category | flops | bytes accessed | tf_op | source)
XLA Modules:
  0.0 89.7 jit_solution(11495981507257958642)
XLA Ops:
  0.7 0.1 multiply_cosine_fusion
  0.8 0.1 pad_maximum_fusion
  0.9 0.6 broadcast_in_dim.8.old_table_ref
  1.5 75.4 %exchange.1 = (bf16[2,576,128]{2,1,0:T(8,128)(2,1)}, f32[3,384,256]{2,1,0:T(8,128)}, s32[8,3072]{1,0:T(8,128)}, f32[640,8]{1,0:T(8,128)}, s32[1,8]{1,0:T(1,128)}, /*index=5*/bf16[16,384,256]{2,1,0:T(8,128)(2,1)}) custom-call(s32[8,16]{1,0:T(8,128)} %bitcast.6, s32[1]{0:T(128)S(6)} %copy.8.count_sm, s32[1,576]{1,0:T(1,128)} %pos_sm.1, ...), custom_call_target="tpu_custom_call" | custom-call | flops 3000000000 | bytes 10000000 | tf_op jit(solution)/shard_map/exchange/pallas_call | solution.py:509
  76.9 12.8 %attend.1 = bf16[576,256]{1,0:T(8,128)(2,1)} custom-call(s32[1,8]{1,0:T(1,128)} %get-tuple-element.11.slots_sm, s32[1,576]{1,0:T(1,128)} %pos_sm.1, s32[1]{0:T(128)S(6)} %copy.8.count_sm, bf16[2,576,128]{2,1,0:T(8,128)(2,1)} %get-tuple-element.12.q_hbm, f32[3,384,256]{2,1,0:T(8,128)} %get-tuple-element.13.acc_hbm, s32[8,3072]{1,0:T(8,128)} %get-tuple-element.14.marks_hbm, ...), custom_call_target="tpu_custom_call" | custom-call | flops 2000000000 | bytes 5000000 | tf_op jit(solution)/shard_map/attend/pallas_call | solution.py:115
  (2 shorter events, 0.0 us)

commit v4 on v3

--- a/solution.py
+++ b/solution.py
@@ -145,7 +145,8 @@
 FLOWS = 6
 KV_PARTS = ((0, 80), (80, 64))
 SIZES = (144, 144, 144, 144, 80, 64)
-ORDER = (4, 5, 0, 2, 1, 3)
+ORDER = (0, 2, 1, 3)
+KV_ORDER = (4, 5)
 ROUTES = ((1, 1), (3, 0), (2, 1), (1, 0), (3, 1), (2, 0), (0, 1))
 SHARE = ROWS // QUERY_FLOWS
 STEPS = 7
@@ -155,7 +156,7 @@
 def exchange_kernel(
     ids_ref, count_sm, pos_ref, hidden_ref, query_ref, keyvalue_ref, cache_ref,
     queries_ref, begun_ref, marks_ref, meta_ref, slots_ref, incoming_ref,
-    ids_sm, held, weights, kv_own, pool, outgoing, sending, arriving, partial, squares, fresh, places,
+    ids_sm, held, weights, kv_own, pool, outgoing, sending, arriving, partial, kv_partial, squares, fresh, places,
     q_raw, table_ref, nk_s, nv_s,
     local_sem, h_send, h_recv, z_send, z_recv, k_send, k_recv,
     x_send, x_recv, f_send, f_recv, d_send, d_recv, r_send, r_recv,
@@ -341,30 +342,35 @@
         return slot
 
     def add_up(s):
-        for way, (offset, size) in enumerate(KV_PARTS):
+        for way in range(2):
             slot = slot_of(way == 0, s)
-            to = (z + 15 - s) % 8 if way == 0 else (z + 1 + s) % 8
             rows = pl.ds(way * 2 * SHARE, 2 * SHARE)
-            kv_rows = pl.ds(pl.multiple_of((to % 4) * SHARE + offset, 16), size)
             total = jnp.zeros((2 * SHARE, 256), jnp.float32)
             for b in range(2):
                 total += jnp.dot(held[b, rows], weights[slot, b], preferred_element_type=jnp.float32)
-            partial[way, : 2 * SHARE] = total
-            partial[way, 2 * SHARE : 2 * SHARE + size] = jnp.dot(
+            partial[way] = total
+
+    def add_up_kv(s, carry):
+        for way, (offset, size) in enumerate(KV_PARTS):
+            to = (z + 15 - s) % 8 if way == 0 else (z + 1 + s) % 8
+            kv_rows = pl.ds(pl.multiple_of((to % 4) * SHARE + offset, 16), size)
+            kv_partial[s, offset : offset + size] = jnp.dot(
                 held[low, kv_rows], kv_own[to // 4], preferred_element_type=jnp.float32
             ) + jnp.dot(
                 held[1 - low, kv_rows],
                 weights[KV_SLOT, to // 4],
                 preferred_element_type=jnp.float32,
             )
+        return carry
 
     def is_up(f):
         return f in (0, 1, 4)
 
-    def part_of(f):
+    def part_of(f, s):
         if f < QUERY_FLOWS:
             return partial[f // 2, f % 2 * SHARE : (f % 2 + 1) * SHARE]
-        return partial[f - QUERY_FLOWS, 2 * SHARE : 2 * SHARE + SIZES[f]]
+        offset, size = KV_PARTS[f - QUERY_FLOWS]
+        return kv_partial[s, offset : offset + size]
 
     def hop(f, s):
         to = (z + 1) % 8 if is_up(f) else (z + 7) % 8
@@ -378,24 +384,30 @@
         sending[f, s, : SIZES[f]] = total.astype(jnp.bfloat16)
         hop(f, s).start()
 
+    def summed(f, s):
+        hop(f, s).wait_recv()
+        return part_of(f, s + 1) + arriving[f, s, : SIZES[f]].astype(jnp.float32)
+
+    def relay(s, flows=ORDER):
+        for f in flows:
+            forward(f, s, summed(f, s - 1))
+
+    add_up_kv(0, 0)
+    for f in KV_ORDER:
+        forward(f, 0, part_of(f, 0))
     add_up(0)
     for f in ORDER:
-        forward(f, 0, part_of(f))
+        forward(f, 0, part_of(f, 0))
     third(1)
+    lax.fori_loop(1, STEPS + 1, add_up_kv, 0)
+    relay(1, KV_ORDER)
     second(3)
     for copy in passages:
         copy.start()
     fourth(1)
     add_up(1)
 
-    def summed(f, s):
-        hop(f, s).wait_recv()
-        return part_of(f) + arriving[f, s, : SIZES[f]].astype(jnp.float32)
-
-    def relay(s):
-        for f in ORDER:
-            forward(f, s, summed(f, s - 1))
-
+    relay(2, KV_ORDER)
     relay(1)
     third(2)
     third(3)
@@ -420,16 +432,19 @@
     for copy in sums:
         copy.start()
 
+    relay(3, KV_ORDER)
     relay(2)
     fourth(3)
     add_up(3)
-
-    def step(s, carry):
-        relay(s)
-        add_up(s + 1)
-        return carry
-
-    lax.fori_loop(3, STEPS, step, 0)
+    relay(4, KV_ORDER)
+    relay(3)
+    add_up(4)
+    relay(5, KV_ORDER)
+    relay(4)
+    add_up(5)
+    relay(6, KV_ORDER)
+    relay(5)
+    add_up(6)
     for f in range(QUERY_FLOWS, FLOWS):
         offset, size = KV_PARTS[f - QUERY_FLOWS]
         fresh[quarter, offset : offset + size] = summed(f, STEPS - 1).astype(jnp.bfloat16)
@@ -439,8 +454,10 @@
     ) for d in range(1, 4)]
     for copy in shared:
         copy.start()
-    for f in ORDER[2:]:
-        q_raw[f * SHARE : (f + 1) * SHARE] = summed(f, STEPS - 1)
+    relay(6)
+    add_up(STEPS)
+    heads = q_raw.shape[1] // HEAD_DIM
+    scale = HEAD_DIM**-0.5 * math.log2(math.e)
     for copy in sums:
         copy.wait_recv()
     total = squares[0]
@@ -451,12 +468,6 @@
     meta = jnp.transpose(jnp.where(first_row, inverse, places[...]))
     meta_ref[...] = meta
     inverse = meta[:ROWS, :1]
-    heads = q_raw.shape[1] // HEAD_DIM
-    scale = HEAD_DIM**-0.5 * math.log2(math.e)
-    for h in range(heads):
-        part = q_raw[:, h * HEAD_DIM : (h + 1) * HEAD_DIM] * inverse
-        part = turned(part, table_ref[:, :HEAD_DIM], table_ref[:, HEAD_DIM:])
-        queries_ref[h] = (part * scale).astype(jnp.bfloat16)
     for copy in shared:
         copy.wait_recv()
     for i in range(4):
@@ -465,6 +476,12 @@
         key = turned(key_value[:, :HEAD_DIM], table_ref[rows, :HEAD_DIM], table_ref[rows, HEAD_DIM:])
         nk_s[rows] = key.astype(jnp.bfloat16)
         nv_s[rows, :HEAD_DIM] = key_value[:, HEAD_DIM:].astype(jnp.bfloat16)
+    for f in ORDER:
+        q_raw[f * SHARE : (f + 1) * SHARE] = summed(f, STEPS - 1)
+    for h in range(heads):
+        part = q_raw[:, h * HEAD_DIM : (h + 1) * HEAD_DIM] * inverse
+        part = turned(part, table_ref[:, :HEAD_DIM], table_ref[:, HEAD_DIM:])
+        queries_ref[h] = (part * scale).astype(jnp.bfloat16)
     for b in range(ROWS // BLOCK):
         begin, end = b * BLOCK, (b + 1) * BLOCK
         width = -(-end // 128) * 128
@@ -527,7 +544,8 @@
             pltpu.VMEM((16, PASSAGE, 256), jnp.bfloat16),
             pltpu.VMEM((FLOWS, STEPS, SHARE, 256), jnp.bfloat16),
             pltpu.VMEM((FLOWS, STEPS, SHARE, 256), jnp.bfloat16),
-            pltpu.VMEM((2, 2 * SHARE + 80, 256), jnp.float32),
+            pltpu.VMEM((2, 2 * SHARE, 256), jnp.float32),
+            pltpu.VMEM((STEPS + 1, SHARE, 256), jnp.float32),
             pltpu.VMEM((8, 8, 640), jnp.float32),
             pltpu.VMEM((4, SHARE, 256), jnp.bfloat16),
             pltpu.VMEM((8, 640), jnp.float32),

time: 91 us -> 90.5 us (level)
  no operation moved by 1% of the time
where the time goes in v4:
time: 90.5 us; the launch traced here: 89.9 us
  Pallas kernels  88.4 us (98%)
    pallas_call x1, Pallas kernels, exchange(): pl.pallas_call(exchange_kernel, out_shape=(jax.ShapeDtypeStruct((2, ROWS,...  75.6 us
    pallas_call x1, Pallas kernels, attend(): pl.pallas_call(attend_kernel, out_shape=jax.ShapeDtypeStruct((ROWS, heads...  12.8 us

profile of v4, /device:TPU:2, one launch (start us, length us, event | category | flops | bytes accessed | tf_op | source)
XLA Modules:
  0.0 89.9 jit_solution(18229736759250145907)
XLA Ops:
  0.7 0.1 multiply_cosine_fusion
  0.8 0.1 pad_maximum_fusion
  0.9 0.6 broadcast_in_dim.8.old_table_ref
  1.5 75.6 %exchange.1 = (bf16[2,576,128]{2,1,0:T(8,128)(2,1)}, f32[3,384,256]{2,1,0:T(8,128)}, s32[8,3072]{1,0:T(8,128)}, f32[640,8]{1,0:T(8,128)}, s32[1,8]{1,0:T(1,128)}, /*index=5*/bf16[16,384,256]{2,1,0:T(8,128)(2,1)}) custom-call(s32[8,16]{1,0:T(8,128)} %bitcast.6, s32[1]{0:T(128)S(6)} %copy.8.count_sm, s32[1,576]{1,0:T(1,128)} %pos_sm.1, ...), custom_call_target="tpu_custom_call" | custom-call | flops 3000000000 | bytes 10000000 | tf_op jit(solution)/shard_map/exchange/pallas_call | solution.py:526
  77.1 12.8 %attend.1 = bf16[576,256]{1,0:T(8,128)(2,1)} custom-call(s32[1,8]{1,0:T(1,128)} %get-tuple-element.11.slots_sm, s32[1,576]{1,0:T(1,128)} %pos_sm.1, s32[1]{0:T(128)S(6)} %copy.8.count_sm, bf16[2,576,128]{2,1,0:T(8,128)(2,1)} %get-tuple-element.12.q_hbm, f32[3,384,256]{2,1,0:T(8,128)} %get-tuple-element.13.acc_hbm, s32[8,3072]{1,0:T(8,128)} %get-tuple-element.14.marks_hbm, ...), custom_call_target="tpu_custom_call" | custom-call | flops 2000000000 | bytes 5000000 | tf_op jit(solution)/shard_map/attend/pallas_call | solution.py:115
  (2 shorter events, 0.0 us)

commit v5 on v3

--- a/solution.py
+++ b/solution.py
@@ -37,7 +37,8 @@
 
 def attend_kernel(
     slots_sm, pos_sm, count_sm, q_hbm, acc_hbm, marks_hbm, meta_hbm, old_table_ref, incoming_hbm,
-    out_ref, q_s, acc_in, kp_s, meta_ref, old_ref, kk_s, vv_s, acc_s, sem, old_sem,
+    out_hbm, out_ref, q_s, acc_in, kp_s, meta_ref, old_ref, kk_s, vv_s, acc_s,
+    sem, old_sem, out_sem,
 ):
     heads = q_s.shape[0]
     olds = [
@@ -64,6 +65,7 @@
         vv_s[rows, :HEAD_DIM] = block[:, HEAD_DIM:]
     for copy in fetched:
         copy.wait()
+    leaving = []
     for b in range(ROWS // BLOCK):
         low, high = b * BLOCK, (b + 1) * BLOCK
 
@@ -105,6 +107,14 @@
                 piece = jnp.where(live, result[h * BLOCK : (h + 1) * BLOCK], 0.0)
                 out_ref[low:high, h * HEAD_DIM : (h + 1) * HEAD_DIM] = piece.astype(jnp.bfloat16)
 
+        rows = pl.ds(low, BLOCK)
+        leaving.append(
+            pltpu.make_async_copy(out_ref.at[rows], out_hbm.at[rows], out_sem.at[b])
+        )
+        leaving[b].start()
+    for copy in leaving:
+        copy.wait()
+
 
 def attend(slots, select_index, select_count, queries, begun, marks, meta, incoming):
     heads = queries.shape[0]
@@ -116,8 +126,9 @@
         attend_kernel,
         out_shape=jax.ShapeDtypeStruct((ROWS, heads * HEAD_DIM), jnp.bfloat16),
         in_specs=[smem] * 3 + [hbm] * 4 + [vmem, hbm],
-        out_specs=vmem,
+        out_specs=hbm,
         scratch_shapes=[
+            pltpu.VMEM((ROWS, heads * HEAD_DIM), jnp.bfloat16),
             pltpu.VMEM(queries.shape, queries.dtype),
             pltpu.VMEM(begun.shape, begun.dtype),
             pltpu.VMEM(marks.shape, marks.dtype),
@@ -128,6 +139,7 @@
             pltpu.VMEM((heads * BLOCK, 2 * HEAD_DIM), jnp.float32),
             pltpu.SemaphoreType.DMA((4,)),
             pltpu.SemaphoreType.DMA((PASSAGES,)),
+            pltpu.SemaphoreType.DMA((ROWS // BLOCK,)),
         ],
         name="attend",
         cost_estimate=pl.CostEstimate(flops=2 * 10**9, bytes_accessed=5 * 10**6, transcendentals=0),

time: 91 us -> 91.8 us (level)
  the two profiles are of different devices: /device:TPU:2 before, /device:TPU:32 now
where the time goes in v5:
time: 91.8 us; the launch traced here: 92.1 us
  Pallas kernels  90.6 us (99%)
    pallas_call x1, Pallas kernels, exchange(): pl.pallas_call(exchange_kernel, out_shape=(jax.ShapeDtypeStruct((2, ROWS,...  76.9 us
    pallas_call x1, Pallas kernels, attend(): pl.pallas_call(attend_kernel, out_shape=jax.ShapeDtypeStruct((ROWS, heads...  13.7 us

profile of v5, /device:TPU:32, one launch (start us, length us, event | category | flops | bytes accessed | tf_op | source)
XLA Modules:
  0.0 92.1 jit_solution(13453000620859360928)
XLA Ops:
  0.7 0.1 multiply_cosine_fusion
  0.8 0.1 pad_maximum_fusion
  0.9 0.6 broadcast_in_dim.8.old_table_ref
  1.5 76.9 %exchange.1 = (bf16[2,576,128]{2,1,0:T(8,128)(2,1)}, f32[3,384,256]{2,1,0:T(8,128)}, s32[8,3072]{1,0:T(8,128)}, f32[640,8]{1,0:T(8,128)}, s32[1,8]{1,0:T(1,128)}, /*index=5*/bf16[16,384,256]{2,1,0:T(8,128)(2,1)}) custom-call(s32[8,16]{1,0:T(8,128)} %bitcast.6, s32[1]{0:T(128)S(6)} %copy.8.count_sm, s32[1,576]{1,0:T(1,128)} %pos_sm.1, ...), custom_call_target="tpu_custom_call" | custom-call | flops 3000000000 | bytes 10000000 | tf_op jit(solution)/shard_map/exchange/pallas_call | solution.py:521
  78.4 13.7 %attend.1 = bf16[576,256]{1,0:T(8,128)(2,1)} custom-call(s32[1,8]{1,0:T(1,128)} %get-tuple-element.11.slots_sm, s32[1,576]{1,0:T(1,128)} %pos_sm.1, s32[1]{0:T(128)S(6)} %copy.8.count_sm, bf16[2,576,128]{2,1,0:T(8,128)(2,1)} %get-tuple-element.12.q_hbm, f32[3,384,256]{2,1,0:T(8,128)} %get-tuple-element.13.acc_hbm, s32[8,3072]{1,0:T(8,128)} %get-tuple-element.14.marks_hbm, ...), custom_call_target="tpu_custom_call" | custom-call | flops 2000000000 | bytes 5000000 | tf_op jit(solution)/shard_map/attend/pallas_call | solution.py:125
  (2 shorter events, 0.0 us)
